TPU v7x, 32 devices: a whole 2x2x4 slice. The times are simulated.
32 devices in a mesh: proto: 8 (over z, y), data: 4 (over x, core).
Axes of the slice: x: 2, y: 2, z: 4, core: 2. Of those that a mesh axis runs over, the one named last changes fastest.
Arguments:
- emb_one: bfloat16 [2048, 256], P('data')
- emb_two: bfloat16 [2048, 256], P('data')
- protos: bfloat16 [4096, 256], P('proto')
Outputs:
- output 1: float32 [2048, 4096], P('data', 'proto')
- output 2: float32 [2048, 4096], P('data', 'proto')
- output 3: float32 [], replicated
- output 4: float32 [2048, 256], P('data')
- output 5: float32 [2048, 256], P('data')
- output 6: float32 [4096, 256], P('proto')
All inputs are finite; a program needn't handle non-finite values.
Results may differ from a plain program's by a relative error of at most 0.001.
Values are sent between devices in bfloat16 or wider.
A program may use at most 1 GiB of HBM per device.

v0:
```python
import jax
import jax.numpy as jnp
from jax import lax
from jax.sharding import PartitionSpec as P, NamedSharding

EPSILON = 0.05
TEMP_TAU = 0.1
value_a14 = 3


def solution(mesh):
    proto_size = mesh.shape['proto']
    data_size = mesh.shape['data']

    def local_step(emb_one, emb_two, protos):
        local_rows = emb_one.shape[0]
        total_rows = local_rows * data_size
        total_protos = protos.shape[0] * proto_size

        def view_terms(emb):
            scores = jnp.einsum('nd,kd->nk', emb, protos, preferred_element_type=jnp.float32)
            transport = jnp.exp(scores / EPSILON)
            for _ in range(value_a14):
                col_sum = lax.psum(jnp.sum(transport, axis=0), 'data')
                transport = transport / (total_protos * col_sum)
                row_sum = lax.psum(jnp.sum(transport, axis=1, keepdims=True), 'proto')
                transport = transport / (total_rows * row_sum)
            codes = total_rows * transport
            logits = scores / TEMP_TAU
            soft_denom = lax.psum(jnp.sum(jnp.exp(logits), axis=1, keepdims=True), 'proto')
            return codes, logits - jnp.log(soft_denom)

        codes_one, logp_one = view_terms(emb_one)
        codes_two, logp_two = view_terms(emb_two)
        part_loss = jnp.sum(codes_two * logp_one) + jnp.sum(codes_one * logp_two)
        loss_value = -lax.psum(part_loss, ('proto', 'data')) / (2 * total_rows)
        grad_scale = 2 * total_rows * TEMP_TAU
        logit_grad_one = ((jnp.exp(logp_one) - codes_two) / grad_scale).astype(jnp.bfloat16)
        logit_grad_two = ((jnp.exp(logp_two) - codes_one) / grad_scale).astype(jnp.bfloat16)
        grad_one = lax.psum(jnp.einsum('nk,kd->nd', logit_grad_one, protos, preferred_element_type=jnp.float32), 'proto')
        grad_two = lax.psum(jnp.einsum('nk,kd->nd', logit_grad_two, protos, preferred_element_type=jnp.float32), 'proto')
        proto_part = (jnp.einsum('nk,nd->kd', logit_grad_one, emb_one, preferred_element_type=jnp.float32)
                      + jnp.einsum('nk,nd->kd', logit_grad_two, emb_two, preferred_element_type=jnp.float32))
        grad_protos = lax.psum(proto_part, 'data')
        return codes_one, codes_two, loss_value, grad_one, grad_two, grad_protos

    return jax.shard_map(
        local_step, mesh=mesh,
        in_specs=(P('data', None), P('data', None), P('proto', None)),
        out_specs=(P('data', 'proto'), P('data', 'proto'), P(), P('data', None), P('data', None), P('proto', None)),
        check_vma=False)
```

profile of v0, /device:TPU:1, one launch (start us, length us, event | category | flops | bytes accessed | tf_op | source)
XLA Modules:
  0.0 288.1 jit_solution(15539497970687072790)
XLA Ops:
  7.2 0.0 copy-start
  7.2 0.0 all-reduce.7.cloned.1.call-start
  7.2 0.9 copy-done
  8.1 1.4 fusion.24
  9.5 6.4 %psum.126 = f32[512]{0:T(512)S(1)} all-reduce(f32[512]{0:T(512)S(1)} %get-tuple-element.36), channel_id=1, replica_groups=mesh['proto'=8,'data'=4] {'data'}, use_global_device_ids=true, to_apply=%region_1.0 | all-reduce | flops 512 | bytes 4096 | tf_op jit(solution)/shard_map/psum | solution.py:24
  15.9 0.3 exponential_reduce_fusion.1
  16.2 18.1 %psum.127 = f32[512,1]{0,1:T(1,128)S(1)} all-reduce(f32[512,1]{0,1:T(1,128)S(1)} %bitcast.53), channel_id=1, replica_groups=mesh['proto'=8,'data'=4] {'proto'}, use_global_device_ids=true, to_apply=%region_3.0 | all-reduce | flops 512 | bytes 4096 | tf_op jit(solution)/shard_map/psum | solution.py:26
  34.3 0.4 fusion.16
  34.7 10.7 %psum.128 = f32[512]{0:T(512)S(1)} all-reduce(f32[512]{0:T(512)S(1)} %fusion.16), channel_id=1, replica_groups=mesh['proto'=8,'data'=4] {'data'}, use_global_device_ids=true, to_apply=%region_5.0 | all-reduce | flops 512 | bytes 4096 | tf_op jit(solution)/shard_map/psum | solution.py:24
  45.3 0.3 fusion.19
  45.7 13.7 %psum.129 = f32[512,1]{0,1:T(1,128)S(1)} all-reduce(f32[512,1]{0,1:T(1,128)S(1)} %bitcast.54), channel_id=1, replica_groups=mesh['proto'=8,'data'=4] {'proto'}, use_global_device_ids=true, to_apply=%region_7.0 | all-reduce | flops 512 | bytes 4096 | tf_op jit(solution)/shard_map/psum | solution.py:26
  59.3 0.0 copy-start.9
  59.3 0.5 fusion.20
  59.8 0.5 copy-done.9
  60.3 0.6 exponential_reduce_fusion
  60.8 9.3 %all-reduce.3 = (f32[512]{0:T(512)S(1)}, f32[512]{0:T(512)S(1)}) all-reduce(f32[512]{0:T(512)S(1)} %fusion.20, f32[512]{0:T(512)S(1)} %get-tuple-element.21), channel_id=1, replica_groups=mesh['proto'=8,'data'=4] {'data'}, use_global_device_ids=true, to_apply=%region_9.0 | all-reduce | flops 1024 | bytes 8192 | tf_op jit(solution)/shard_map/psum | solution.py:24
  70.2 0.4 fusion.23
  70.6 15.4 %all-reduce.1 = (f32[512,1]{0,1:T(1,128)S(1)}, f32[512,1]{0,1:T(1,128)S(1)}) all-reduce(f32[512,1]{0,1:T(1,128)S(1)} %bitcast.52, f32[512,1]{0,1:T(1,128)S(1)} %bitcast.57), channel_id=1, replica_groups=mesh['proto'=8,'data'=4] {'proto'}, use_global_device_ids=true, to_apply=%region_11.0 | all-reduce | flops 1024 | bytes 8192 | tf_op jit(solution)/shard_map/psum | solution.py:26
  86.0 1.4 multiply_convert_fusion
  87.4 0.9 multiply_reduce_fusion
  88.4 13.6 %psum.133 = f32[512,1]{0,1:T(1,128)S(1)} all-reduce(f32[512,1]{0,1:T(1,128)S(1)} %bitcast.56), channel_id=1, replica_groups=mesh['proto'=8,'data'=4] {'proto'}, use_global_device_ids=true, to_apply=%region_15.0 | all-reduce | flops 512 | bytes 4096 | tf_op jit(solution)/shard_map/psum | solution.py:26
  102.0 0.4 fusion.17
  102.4 13.0 %psum.134 = f32[512]{0:T(512)S(1)} all-reduce(f32[512]{0:T(512)S(1)} %fusion.17), channel_id=1, replica_groups=mesh['proto'=8,'data'=4] {'data'}, use_global_device_ids=true, to_apply=%region_17.0 | all-reduce | flops 512 | bytes 4096 | tf_op jit(solution)/shard_map/psum | solution.py:24
  115.4 0.3 fusion.18
  115.7 15.4 %psum.135 = f32[512,1]{0,1:T(1,128)S(1)} all-reduce(f32[512,1]{0,1:T(1,128)S(1)} %bitcast.55), channel_id=1, replica_groups=mesh['proto'=8,'data'=4] {'proto'}, use_global_device_ids=true, to_apply=%region_19.0 | all-reduce | flops 512 | bytes 4096 | tf_op jit(solution)/shard_map/psum | solution.py:26
  131.1 0.5 fusion.21
  131.6 9.5 %psum.136 = f32[512]{0:T(512)S(1)} all-reduce(f32[512]{0:T(512)S(1)} %fusion.21), channel_id=1, replica_groups=mesh['proto'=8,'data'=4] {'data'}, use_global_device_ids=true, to_apply=%region_21.0 | all-reduce | flops 512 | bytes 4096 | tf_op jit(solution)/shard_map/psum | solution.py:24
  141.1 0.4 fusion.22
  141.5 13.7 %all-reduce = (f32[512,1]{0,1:T(1,128)S(1)}, f32[512,1]{0,1:T(1,128)S(1)}) all-reduce(f32[512,1]{0,1:T(1,128)S(1)} %bitcast.51, f32[512,1]{0,1:T(1,128)S(1)} %bitcast.48), channel_id=1, replica_groups=mesh['proto'=8,'data'=4] {'proto'}, use_global_device_ids=true, to_apply=%region_23.0 | all-reduce | flops 1024 | bytes 8192 | tf_op jit(solution)/shard_map/psum | solution.py:26
  155.2 0.0 copy-start.6
  155.2 1.6 multiply_convert_fusion.1
  156.8 0.0 copy-start.4
  156.8 0.0 copy-done.6
  156.8 0.0 copy-start.2
  156.8 0.0 copy-start.10
  156.8 0.3 fusion.30
  157.1 0.5 copy-done.4
  157.6 0.4 copy-done.2
  158.0 0.1 copy-done.10
  158.1 1.1 convolution_add_fusion
  159.2 0.0 copy-start.5
  159.2 0.0 all-reduce.7.cloned.1.call-update
  159.2 0.0 all-reduce.9.cloned.1.call-start
  159.2 1.0 copy-done.5
  160.2 0.0 copy-start.3
  160.2 1.1 fusion.28
  161.4 0.0 copy-done.3
  161.4 0.0 copy-start.1
  161.4 1.1 fusion.29
  162.5 0.0 all-reduce.9.cloned.1.call-update
  162.5 0.1 copy-done.1
  162.6 0.9 multiply_reduce_fusion.1
  164.8 39.9 %psum.140 = f32[]{:T(128)} all-reduce(f32[]{:T(128)S(6)} %add.42), channel_id=1, replica_groups=mesh['proto'=8,'data'=4] {'proto','data'}, use_global_device_ids=true, to_apply=%region_30.0 | all-reduce | flops 1 | bytes 8 | tf_op jit(solution)/shard_map/psum | solution.py:36
  204.7 1.3 copy.11
  206.0 1.3 copy.12
  208.0 0.0 all-reduce.7.cloned.1.call-done
  208.0 68.2 %all-reduce.9.cloned.1.call-done = (f32[512,256]{1,0:T(8,128)}, f32[512,256]{1,0:T(8,128)}) async-done(((f32[512,256]{1,0:T(8,128)}, f32[512,256]{1,0:T(8,128)}), (f32[512,256]{1,0:T(8,128)}, f32[512,256]{1,0:T(8,128)})) %all-reduce.9.cloned.1.call-update) | async-done | bytes 1048592 | tf_op jit(solution)/shard_map/psum | solution.py:40
  276.2 0.0 copy-start.8
  276.2 1.9 copy.16
  278.1 0.0 copy-done.8
  278.1 0.0 copy-start.7
  278.1 0.8 copy.17
  278.9 0.4 copy-done.7
  279.3 0.8 copy.18
  (13 shorter events, 0.1 us)
Async XLA Ops:
  7.2 1.0 copy-start
  7.2 200.8 %all-reduce.7.cloned.1.call-start = ((), (), s32[]{:S(2)}) async-start(), calls=%async_computation | async-start | bytes 1048576 | tf_op jit(solution)/shard_map/psum | solution.py:44
  59.3 1.0 copy-start.9
  155.2 1.6 copy-start.6
  156.8 0.8 copy-start.4
  156.8 1.2 copy-start.2
  156.8 1.3 copy-start.10
  159.2 1.0 copy-start.5
  159.2 117.0 %all-reduce.9.cloned.1.call-start = ((), (), s32[]{:S(2)}) async-start(), calls=%async_computation.1 | async-start | bytes 2097152 | tf_op jit(solution)/shard_map/psum | solution.py:40
  160.2 1.1 copy-start.3
  161.4 1.2 copy-start.1
  276.2 1.9 copy-start.8
  278.1 1.2 copy-start.7
Sparse Core Ops, SparseCore 0:
  159.3 33.0 all-reduce.6
  196.5 79.5 all-reduce.8
where the time goes:
time: 290 us; the launch traced here: 288 us
  blocking collectives  179 us (62%)
  waiting for transfers between devices  68.2 us (24%)
  between operations  17.2 us (6%)
  local copies, waits for them, and re-layouts  10 us (3%)
  other arithmetic  8.46 us (3%)
  matrix products  5.58 us (2%)
    psum x6, blocking collectives, view_terms(): row_sum = lax.psum(jnp.sum(transport, axis=1, keepdims=True), 'proto')  89.8 us
    psum x1, waiting for transfers between devices, local_step(): lax.psum(jnp.einsum('nk,kd->nd', logit_grad_one, protos, preferred_elemen...  68.2 us
    psum x5, blocking collectives, view_terms(): col_sum = lax.psum(jnp.sum(transport, axis=0), 'data')  48.9 us
    psum x1, blocking collectives, local_step(): loss_value = -lax.psum(part_loss, ('proto', 'data')) / (2 * total_rows)  39.9 us
    unnamed x27, local copies, waits for them, and re-layouts  10 us
  transfers between devices with their start and end apart: 2, of which 1 were waited for; matrix products, arithmetic and copies ran while one was open for 2% of the time, Pallas kernels for 0%

commit v1 on v0

v1 whole, which is shorter than its diff:
```python
import functools
import math

import jax
import jax.numpy as jnp
from jax import lax
from jax.experimental import pallas as pl
from jax.experimental.pallas import tpu as pltpu
from jax.sharding import PartitionSpec as P

TEMP_TAU = 0.1
ITERS = 3
F32, BF16 = jnp.float32, jnp.bfloat16
LOG2E_TAU = math.log2(math.e) / TEMP_TAU
LN2 = math.log(2.0)
B = 512
L = 128
CH = 64
NT = (((1,), (1,)), ((), ()))


def eye_mask():
    return lax.broadcasted_iota(jnp.int32, (L, L), 0) == lax.broadcasted_iota(jnp.int32, (L, L), 1)


def col_to_row(eye, col):
    return jnp.sum(jnp.where(eye, col, 0.0), axis=0, keepdims=True)


def row_to_col(eye, row):
    return jnp.sum(jnp.where(eye, row, 0.0), axis=1, keepdims=True)


def sinkhorn_kernel(np_, nd, z1, z2, c, zall, call, rowv, vvec,
                    T, A, vrep, ctx, crx, rtx, rrx, utx,
                    lsem, cs, cr, rs, rr, vs, vr, us, ur, zs, zr, gs, gr):
    p = lax.axis_index('proto')
    d = lax.axis_index('data')
    total_rows = nd * B
    total_protos = np_ * B
    core = lax.rem(d, 2)

    loads = [pltpu.make_async_copy(z1, zall.at[0, d], lsem.at[0]),
             pltpu.make_async_copy(z2, zall.at[1, d], lsem.at[1]),
             pltpu.make_async_copy(c, call.at[p], lsem.at[2])]
    for cp in loads:
        cp.start()

    def xor(a, k):
        out = a
        for bit in (1, 2, 4):
            if k & bit:
                has = lax.rem(out // bit, 2)
                out = out + bit - 2 * bit * has
        return out

    dpeers = [xor(d, j) for j in range(nd)]
    ppeers = [xor(p, j) for j in range(np_)]

    bar = pltpu.get_barrier_semaphore()
    for j in range(1, nd):
        pl.semaphore_signal(bar, inc=1, device_id={'proto': p, 'data': dpeers[j]})
    for j in range(1, np_):
        pl.semaphore_signal(bar, inc=1, device_id={'proto': ppeers[j], 'data': d})

    for cp in loads:
        cp.wait()

    def remote(src, dst, ss, rs_, pj, dj):
        return pltpu.make_async_remote_copy(src, dst, ss, rs_, device_id={'proto': ppeers[pj], 'data': dpeers[dj]})

    pend = []

    ZQ = B // 4
    HB = B // 2

    def z_piece(i):
        out = []
        for v in range(2):
            ref = zall.at[v, d, pl.ds(i * ZQ, ZQ)]
            cp = remote(ref, ref, zs.at[0, v, i], zr.at[0, v, i], 0, 2)
            cp.start()
            out.append(cp)
        pend.extend(out)
        return out

    def z_partner(src_d, slot):
        out = []
        for v in range(2):
            ref = zall.at[v, src_d]
            cp = remote(ref, ref, zs.at[slot, v, 0], zr.at[slot, v, 0], 0, 1)
            cp.start()
            out.append(cp)
        pend.extend(out)
        return out

    mine = pl.ds(pl.multiple_of(core * HB, HB), HB)

    def c_send(blk, slot, pj, dj):
        ref = call.at[blk, mine]
        cp = remote(ref, ref, gs.at[slot], gr.at[slot], pj, dj)
        cp.start()
        pend.append(cp)
        return cp

    eye = eye_mask()

    for v in range(2):
        T[v] = lax.dot_general(call[p], zall[v, d], NT, preferred_element_type=F32) * LOG2E_TAU
    crow = [None] * 8
    dsum = [None] * 8
    for v in range(2):
        dacc = [jnp.zeros((8, L), F32) for _ in range(4)]
        cols = []
        for ck in range(B // CH):
            rows = pl.ds(ck * CH, CH)
            part = None
            for j in range(4):
                e = jnp.exp2(T[v, rows, j * L:(j + 1) * L])
                a = e * e
                A[v, rows, j * L:(j + 1) * L] = a
                dacc[j] = dacc[j] + jnp.sum(e.reshape(CH // 8, 8, L), axis=0)
                part = a if part is None else part + a
            cols.append(jnp.sum(part, axis=1, keepdims=True))
        per = L // CH
        for i in range(4):
            crow[4 * v + i] = col_to_row(eye, jnp.concatenate(cols[per * i:per * (i + 1)], axis=0))
            dsum[4 * v + i] = jnp.sum(dacc[i], axis=0, keepdims=True)

    pl.semaphore_wait(bar, nd - 1 + np_ - 1)

    z_recv = []
    u_tile = None
    dfull = None
    for it in range(ITERS):
        for i in range(8):
            ctx[it, i:i + 1] = crow[i]
        cps = []
        for j in range(1, nd):
            cp = remote(ctx.at[it], crx.at[it, j], cs.at[it, j], cr.at[it, j], 0, j)
            cp.start()
            cps.append(cp)
        pend.extend(cps)
        if it == 0:
            zp1 = z_partner(d, 1)
            z_recv += z_piece(0)
            g_y = c_send(p, 0, 1, 0)
            g_z1 = c_send(p, 1, 2, 0)
        elif it == 1:
            z_recv += z_piece(2)
        ctot = ctx[it]
        for j, cp in zip(range(1, nd), cps):
            cp.wait_recv()
            ctot = ctot + crx[it, j]
        vt = 1.0 / (total_protos * ctot)
        if it == ITERS - 1:
            vvec[p] = vt
            vcps = []
            for j in range(1, np_):
                cp = remote(vvec.at[p], vvec.at[p], vs.at[j], vr.at[j], j, 0)
                cp.start()
                vcps.append(cp)
            pend.extend(vcps)
        for v in range(2):
            for i in range(4):
                vrep[v, i * L:(i + 1) * L] = jnp.broadcast_to(row_to_col(eye, vt[4 * v + i:4 * v + i + 1]), (L, L))
        last = it == ITERS - 1
        for v in range(2):
            racc = [jnp.zeros((8, L), F32) for _ in range(4)]
            tacc = [jnp.zeros((8, L), F32) for _ in range(4)]
            for ck in range(B // CH):
                rows = pl.ds(ck * CH, CH)
                w = vrep[v, rows]
                for j in range(4):
                    lanes = slice(j * L, (j + 1) * L)
                    m = A[v, rows, lanes] * w
                    racc[j] = racc[j] + jnp.sum(m.reshape(CH // 8, 8, L), axis=0)
                    if last:
                        mt = m * T[1 - v, rows, lanes]
                        tacc[j] = tacc[j] + jnp.sum(mt.reshape(CH // 8, 8, L), axis=0)
            for j in range(4):
                rtx[it, 4 * v + j:4 * v + j + 1] = jnp.sum(racc[j], axis=0, keepdims=True)
                if last:
                    rtx[it, 8 + 4 * v + j:8 + 4 * v + j + 1] = jnp.sum(tacc[j], axis=0, keepdims=True)
        if it == 0:
            for i in range(8):
                rtx[it, 8 + i:9 + i] = dsum[i]
        nrow = 8 if it == 1 else 16
        cps = []
        for j in range(1, np_):
            cp = remote(rtx.at[it, 0:nrow], rrx.at[it, j, 0:nrow], rs.at[it, j], rr.at[it, j], j, 0)
            cp.start()
            cps.append(cp)
        pend.extend(cps)
        if it == 0:
            z_recv += z_piece(1)
            g_y.wait_recv()
            g_z1.wait_recv()
            g_z2 = c_send(p, 2, 4, 0)
            g_y1 = c_send(ppeers[2], 3, 1, 0)
        elif it == 1:
            z_recv += z_piece(3)
            g_z2.wait_recv()
            g_z3 = c_send(p, 4, 6, 0)
            g_y2 = c_send(ppeers[4], 5, 1, 0)
        else:
            g_z3.wait_recv()
            g_y3 = c_send(ppeers[6], 6, 1, 0)
            for cp in z_recv:
                cp.wait_recv()
            zp2 = z_partner(dpeers[2], 2)
        rtot = rtx[it, 0:nrow]
        for j, cp in zip(range(1, np_), cps):
            cp.wait_recv()
            rtot = rtot + rrx[it, j, 0:nrow]
        if it == 0:
            dfull = rtot[8:16]
        u_tile = 1.0 / (total_rows * rtot[0:8])
        if not last:
            for v in range(2):
                cols = []
                for ck in range(B // CH):
                    rows = pl.ds(ck * CH, CH)
                    part = None
                    for j in range(4):
                        m = A[v, rows, j * L:(j + 1) * L] * u_tile[4 * v + j:4 * v + j + 1]
                        part = m if part is None else part + m
                    cols.append(jnp.sum(part, axis=1, keepdims=True))
                per = L // CH
                for i in range(4):
                    crow[4 * v + i] = col_to_row(eye, jnp.concatenate(cols[per * i:per * (i + 1)], axis=0))
    g_y1.wait_recv()
    g_y2.wait_recv()
    g_y3.wait_recv()
    gp = [c_send(k, 8 + k, 0, 1) for k in range(np_)]

    w = total_rows * u_tile
    logd = jnp.log(dfull)
    swapped = jnp.concatenate([logd[4:8], logd[0:4]], axis=0)
    terms = w * rtot[8:16] * LN2 - (w * rtot[0:8]) * swapped
    tot = jnp.sum(jnp.sum(terms, axis=1, keepdims=True), axis=0, keepdims=True)
    rowv[d, 0:8] = w
    rowv[d, 8:16] = 1.0 / dfull
    rowv[d, 16:24] = jnp.broadcast_to(tot, (8, L))
    ucps = []
    for j in range(1, nd):
        cp = remote(rowv.at[d], rowv.at[d], us.at[j], ur.at[j], 0, j)
        cp.start()
        ucps.append(cp)
    pend.extend(ucps)
    for cp in zp1 + zp2 + gp + ucps + vcps:
        cp.wait_recv()
    for cp in pend:
        cp.wait_send()


def grads_kernel(np_, nd, z1, z2, zall, call, rowv, vvec, q1, q2, loss, g1, g2, gp,
                 T, H, ucol, qbuf, sem):
    p = lax.axis_index('proto')
    d = lax.axis_index('data')
    total_rows = nd * B
    inv_scale = 1.0 / (2 * total_rows * TEMP_TAU)
    eye = eye_mask()
    lsum = rowv[0, 16:17, 0:1]
    for k in range(1, nd):
        lsum = lsum + rowv[k, 16:17, 0:1]
    loss[...] = lsum * (-1.0 / (2 * total_rows))

    for i in range(16):
        ucol[i // 4, (i % 4) * L:(i % 4 + 1) * L] = jnp.broadcast_to(
            row_to_col(eye, rowv[d, i:i + 1]) * inv_scale, (L, L))
    g1[...] = jnp.zeros_like(g1)
    g2[...] = jnp.zeros_like(g2)
    gp[...] = jnp.zeros_like(gp)
    za, zb = zall.at[0, d], zall.at[1, d]

    def scores(k, lhs_rows):
        cb = call[k]
        T[0] = lax.dot_general(za[...], cb, NT, preferred_element_type=F32) * LOG2E_TAU
        T[1] = lax.dot_general(zb[...], cb, NT, preferred_element_type=F32) * LOG2E_TAU

    def block(k, codes):
        scores(k, None)
        vt = vvec[k]
        for ck in range(B // CH):
            rows = pl.ds(ck * CH, CH)
            for j in range(4):
                lanes = slice(j * L, (j + 1) * L)
                e1 = jnp.exp2(T[0, rows, lanes])
                e2 = jnp.exp2(T[1, rows, lanes])
                a1 = (e1 * e1) * vt[j:j + 1] * ucol[0, rows]
                a2 = (e2 * e2) * vt[4 + j:5 + j] * ucol[1, rows]
                H[0, rows, lanes] = (e1 * ucol[2, rows] - a2).astype(BF16)
                H[1, rows, lanes] = (e2 * ucol[3, rows] - a1).astype(BF16)
                if codes:
                    qbuf[0, rows, lanes] = a1 * (1.0 / inv_scale)
                    qbuf[1, rows, lanes] = a2 * (1.0 / inv_scale)
        cb = call[k]
        g1[...] += jnp.dot(H[0], cb, preferred_element_type=F32)
        g2[...] += jnp.dot(H[1], cb, preferred_element_type=F32)

    block(p, True)
    out = [pltpu.make_async_copy(qbuf.at[0], q1, sem.at[0]), pltpu.make_async_copy(qbuf.at[1], q2, sem.at[1])]
    for cp in out:
        cp.start()

    def step(i, carry):
        block(lax.rem(p + i, np_), False)
        return carry

    lax.fori_loop(1, np_, step, 0)

    vt = vvec[p]
    for v in range(2):
        for i in range(4):
            ucol[v, i * L:(i + 1) * L] = jnp.broadcast_to(row_to_col(eye, vt[4 * v + i:4 * v + i + 1]), (L, L))
    cown = call.at[p]

    def cstep(k, carry):
        zk1, zk2 = zall[0, k], zall[1, k]
        T[0] = lax.dot_general(cown[...], zk1, NT, preferred_element_type=F32) * LOG2E_TAU
        T[1] = lax.dot_general(cown[...], zk2, NT, preferred_element_type=F32) * LOG2E_TAU
        rv = rowv[k, 0:16] * inv_scale
        for ck in range(B // CH):
            rows = pl.ds(ck * CH, CH)
            for j in range(4):
                lanes = slice(j * L, (j + 1) * L)
                e1 = jnp.exp2(T[0, rows, lanes])
                e2 = jnp.exp2(T[1, rows, lanes])
                a1 = (e1 * e1) * rv[j:j + 1] * ucol[0, rows]
                a2 = (e2 * e2) * rv[4 + j:5 + j] * ucol[1, rows]
                H[0, rows, lanes] = (e1 * rv[8 + j:9 + j] - a2).astype(BF16)
                H[1, rows, lanes] = (e2 * rv[12 + j:13 + j] - a1).astype(BF16)
        gp[...] += jnp.dot(H[0], zk1, preferred_element_type=F32) + jnp.dot(H[1], zk2, preferred_element_type=F32)
        return carry

    lax.fori_loop(0, nd, cstep, 0)
    for cp in out:
        cp.wait()


def solution(mesh):
    np_ = mesh.shape['proto']
    nd = mesh.shape['data']
    VM = pl.BlockSpec(memory_space=pltpu.VMEM)
    ANY = pl.BlockSpec(memory_space=pl.ANY)
    DMA = pltpu.SemaphoreType.DMA

    def local_step(emb_one, emb_two, protos):
        dim = protos.shape[1]
        zall, call, rowv, vvec = pl.pallas_call(
            functools.partial(sinkhorn_kernel, np_, nd),
            out_shape=(jax.ShapeDtypeStruct((2, nd, B, dim), BF16), jax.ShapeDtypeStruct((np_, B, dim), BF16),
                       jax.ShapeDtypeStruct((nd, 24, L), F32), jax.ShapeDtypeStruct((np_, 8, L), F32)),
            in_specs=[ANY] * 3, out_specs=(VM,) * 4,
            scratch_shapes=[
                pltpu.VMEM((2, B, B), F32), pltpu.VMEM((2, B, B), F32), pltpu.VMEM((2, B, L), F32),
                pltpu.VMEM((ITERS, 8, L), F32), pltpu.VMEM((ITERS, nd, 8, L), F32),
                pltpu.VMEM((ITERS, 16, L), F32), pltpu.VMEM((ITERS, np_, 16, L), F32), pltpu.VMEM((8, L), F32),
                DMA((3,)), DMA((ITERS, nd)), DMA((ITERS, nd)), DMA((ITERS, np_)), DMA((ITERS, np_)),
                DMA((np_,)), DMA((np_,)), DMA((nd,)), DMA((nd,)),
                DMA((3, 2, 4)), DMA((3, 2, 4)), DMA((16,)), DMA((16,))],
            compiler_params=pltpu.CompilerParams(collective_id=0, has_side_effects=True),
            name='sinkhorn',
        )(emb_one, emb_two, protos)
        q1, q2, loss, g1, g2, gp = pl.pallas_call(
            functools.partial(grads_kernel, np_, nd),
            out_shape=(jax.ShapeDtypeStruct((B, B), F32), jax.ShapeDtypeStruct((B, B), F32),
                       jax.ShapeDtypeStruct((1, 1), F32),
                       jax.ShapeDtypeStruct((B, dim), F32), jax.ShapeDtypeStruct((B, dim), F32),
                       jax.ShapeDtypeStruct((B, dim), F32)),
            in_specs=[ANY, ANY] + [VM] * 4, out_specs=(ANY, ANY, VM, VM, VM, VM),
            scratch_shapes=[pltpu.VMEM((2, B, B), F32), pltpu.VMEM((2, B, B), BF16), pltpu.VMEM((4, B, L), F32),
                            pltpu.VMEM((2, B, B), F32), DMA((2,))],
            name='grads',
        )(emb_one, emb_two, zall, call, rowv, vvec)
        return q1, q2, loss.reshape(()), g1, g2, gp

    return jax.shard_map(
        local_step, mesh=mesh,
        in_specs=(P('data', None), P('data', None), P('proto', None)),
        out_specs=(P('data', 'proto'), P('data', 'proto'), P(), P('data', None), P('data', None), P('proto', None)),
        check_vma=False)
```

time: 290 us -> 57.7 us (0.20)
  blocking collectives: 179 us -> 0 us
  waiting for transfers between devices: 68.2 us -> 0 us
  Pallas kernels: 0 us -> 56.9 us
  between operations: 17.2 us -> 0.64 us
  local copies, waits for them, and re-layouts: 10 us -> 0 us
  other arithmetic: 8.46 us -> 0 us
  matrix products: 5.58 us -> 0 us
    psum x12 -> x0, blocking collectives: 179 us -> none  [the longest x6 89.8 us: view_terms(): row_sum = lax.psum(jnp.sum(transport, axis=1, keepdims=True), 'proto')]
    psum x2 -> x0, waiting for transfers between devices: 68.2 us -> none  [the longest x1 68.2 us: local_step(): lax.psum(jnp.einsum('nk,kd->nd', logit_grad_one, protos, preferred_elemen...]
    pallas_call x0 -> x2, Pallas kernels: none -> 56.9 us  [the longest x1 39.4 us: local_step(): pl.pallas_call(functools.partial(sinkhorn_kernel, np_, nd), out_shape=(ja...]
    unnamed x27 -> x0, local copies, waits for them, and re-layouts: 10 us -> none
    dot_general x6 -> x0, matrix products: 5.58 us -> none  [the longest x2 1.93 us: view_terms(): jnp.einsum('nd,kd->nk', emb, protos, preferred_element_type=jnp.float32)]
    reduce_sum x11 -> x0, other arithmetic: 5.34 us -> none  [the longest x2 1.86 us: local_step(): part_loss = jnp.sum(codes_two * logp_one) + jnp.sum(codes_one * logp_two)]
    convert_element_type x2 -> x0, other arithmetic: 3.04 us -> none  [the longest x1 1.61 us: local_step(): ((jnp.exp(logp_one) - codes_two) / grad_scale).astype(jnp.bfloat16)]
  transfers between devices with their start and end apart: 2 -> 0, of which waited for: 1 -> 0; matrix products, arithmetic and copies ran while one was open for 2% -> 0% of each run, Pallas kernels for 0% -> 0%
where the time goes in v1:
time: 57.7 us; the launch traced here: 57.5 us
  Pallas kernels  56.9 us (99%)
  between operations  0.64 us (1%)
    pallas_call x1, Pallas kernels, local_step(): pl.pallas_call(functools.partial(sinkhorn_kernel, np_, nd), out_shape=(ja...  39.4 us
    pallas_call x1, Pallas kernels, local_step(): pl.pallas_call(functools.partial(grads_kernel, np_, nd), out_shape=(jax.S...  17.5 us

profile of v1, /device:TPU:1, one launch (start us, length us, event | category | flops | bytes accessed | tf_op | source)
XLA Modules:
  0.0 57.5 jit_solution(10011460614358827576)
XLA Ops:
  0.6 39.4 %sinkhorn.1 = (bf16[2,4,512,256]{3,2,1,0:T(8,128)(2,1)}, bf16[8,512,256]{2,1,0:T(8,128)(2,1)}, f32[4,24,128]{2,1,0:T(8,128)}, f32[8,8,128]{2,1,0:T(8,128)}) custom-call(bf16[512,256]{1,0:T(8,128)(2,1)} %z1.3, bf16[512,256]{1,0:T(8,128)(2,1)} %z2.3, bf16[512,256]{1,0:T(8,128)(2,1)} %c.1), custom_call_target="tpu_custom_call" | custom-call | tf_op jit(solution)/shard_map/sinkhorn/pallas_call | solution.py:351
  40.1 17.5 %grads.1 = (f32[512,512]{1,0:T(8,128)}, f32[512,512]{1,0:T(8,128)}, f32[1,1]{1,0:T(1,128)}, f32[512,256]{1,0:T(8,128)}, f32[512,256]{1,0:T(8,128)}, /*index=5*/f32[512,256]{1,0:T(8,128)}) custom-call(bf16[512,256]{1,0:T(8,128)(2,1)} %z1.3, bf16[512,256]{1,0:T(8,128)(2,1)} %z2.3, bf16[2,4,512,256]{3,2,1,0:T(8,128)(2,1)} %get-tuple-element.16.zall, ...), custom_call_target="tpu_custom_call" | custom-call | tf_op jit(solution)/shard_map/grads/pallas_call | solution.py:366

commit v2 on v1

v2 whole, which is shorter than its diff:
```python
import functools
import math

import jax
import jax.numpy as jnp
from jax import lax
from jax.experimental import pallas as pl
from jax.experimental.pallas import tpu as pltpu
from jax.sharding import PartitionSpec as P

TEMP_TAU = 0.1
ITERS = 3
F32, BF16 = jnp.float32, jnp.bfloat16
LOG2E_TAU = math.log2(math.e) / TEMP_TAU
LN2 = math.log(2.0)
B = 512
HB = 256
L = 128
CH = 64
NT = (((1,), (1,)), ((), ()))


def eye_mask():
    return lax.broadcasted_iota(jnp.int32, (L, L), 0) == lax.broadcasted_iota(jnp.int32, (L, L), 1)


def col_to_row(eye, col):
    return jnp.sum(jnp.where(eye, col, 0.0), axis=0, keepdims=True)


def row_to_col(eye, row):
    return jnp.sum(jnp.where(eye, row, 0.0), axis=1, keepdims=True)


def xor(a, k):
    out = a
    for bit in (1, 2, 4):
        if k & bit:
            out = out + bit - 2 * bit * lax.rem(out // bit, 2)
    return out


def sinkhorn_kernel(np_, nd, z1, z2, c, zall, call, E, ET, rowv, vvec, vrep,
                    T, A, ctx, crx, rtx, rrx,
                    lsem, cs, cr, rs, rr, vs, vr, us, ur, zs, zr, gs, gr, ds_, dr_):
    p = lax.axis_index('proto')
    d = lax.axis_index('data')
    total_rows = nd * B
    total_protos = np_ * B
    core = lax.rem(d, 2)
    half = core
    other = 1 - core

    loads = [pltpu.make_async_copy(z1.at[h * HB:(h + 1) * HB], zall.at[0, 2 * d + h], lsem.at[h]) for h in range(2)]
    loads += [pltpu.make_async_copy(z2.at[h * HB:(h + 1) * HB], zall.at[1, 2 * d + h], lsem.at[2 + h]) for h in range(2)]
    loads += [pltpu.make_async_copy(c.at[h * HB:(h + 1) * HB], call.at[2 * p + h], lsem.at[4 + h]) for h in range(2)]
    for cp in loads:
        cp.start()

    dp = [xor(d, j) for j in range(nd)]
    pp = [xor(p, j) for j in range(np_)]

    bar = pltpu.get_barrier_semaphore()
    for j in range(1, nd):
        pl.semaphore_signal(bar, inc=1, device_id={'proto': p, 'data': dp[j]})
    for j in range(1, np_):
        pl.semaphore_signal(bar, inc=1, device_id={'proto': pp[j], 'data': d})

    for cp in loads:
        cp.wait()

    pend = []

    def send(src, dst, ss, rs_, pj, dj):
        cp = pltpu.make_async_remote_copy(src, dst, ss, rs_, device_id={'proto': pp[pj], 'data': dp[dj]})
        cp.start()
        pend.append(cp)
        return cp

    def z_x(i):
        ref = zall.at[i // 2, 2 * d + i % 2]
        return send(ref, ref, zs.at[i], zr.at[i], 0, 2)

    def z_partner(slot, v, nb):
        ref = zall.at[v, nb]
        return send(ref, ref, zs.at[slot], zr.at[slot], 0, 1)

    def c_send(slot, q, pj, rows=None):
        ref = call.at[2 * q + half] if rows is None else call.at[2 * q + half, rows]
        return send(ref, ref, gs.at[slot], gr.at[slot], pj, 0)

    def c_partner(j):
        ref = call.at[2 * pp[j] + half]
        return send(ref, ref, ds_.at[j], dr_.at[j], 0, 1)

    def scores_rows(hb):
        def body(v, carry):
            zz = zall[v, pl.ds(2 * d, 2)].reshape(B, -1)
            s = lax.dot_general(zz, call[hb], NT, preferred_element_type=F32)
            E[v, hb] = jnp.exp2(s * LOG2E_TAU)
            return carry
        for v in range(2):
            body(v, 0)

    def scores_cols(nb):
        def body(v, carry):
            cc = call[pl.ds(2 * p, 2)].reshape(B, -1)
            s = lax.dot_general(cc, zall[v, nb], NT, preferred_element_type=F32)
            ET[v, nb] = jnp.exp2(s * LOG2E_TAU)
            return carry
        for v in range(2):
            body(v, 0)

    eye = eye_mask()

    crow = [None] * 8
    dsum = [None] * 8
    for v in range(2):
        for h in range(2):
            for h2 in range(2):
                T[v, h * HB:(h + 1) * HB, h2 * HB:(h2 + 1) * HB] = lax.dot_general(
                    call[2 * p + h], zall[v, 2 * d + h2], NT, preferred_element_type=F32) * LOG2E_TAU

    per = L // CH

    def finish_cols(v, cols):
        for i in range(4):
            crow[4 * v + i] = col_to_row(eye, jnp.concatenate(cols[per * i:per * (i + 1)], axis=0))

    for v in range(2):
        dacc = [jnp.zeros((8, L), F32) for _ in range(4)]
        cols = []
        for ck in range(B // CH):
            rows = pl.ds(ck * CH, CH)
            part = None
            for j in range(4):
                e = jnp.exp2(T[v, rows, j * L:(j + 1) * L])
                a = e * e
                ET[v, 2 * d + j // 2, rows, (j % 2) * L:(j % 2 + 1) * L] = e
                A[v, rows, j * L:(j + 1) * L] = a
                dacc[j] = dacc[j] + jnp.sum(e.reshape(CH // 8, 8, L), axis=0)
                part = a if part is None else part + a
            cols.append(jnp.sum(part, axis=1, keepdims=True))
        finish_cols(v, cols)
        for j in range(4):
            dsum[4 * v + j] = jnp.sum(dacc[j], axis=0, keepdims=True)

    pl.semaphore_wait(bar, nd - 1 + np_ - 1)

    bulk = {}
    QR = [pl.ds(0, L), pl.ds(L, L)]

    def background(it, along_data):
        if it == 0 and along_data:
            for v in range(2):
                for h in range(2):
                    bulk['zp', v, h] = z_partner(4 + 2 * v + h, v, 2 * d + h)
            bulk['zx', 0] = z_x(0)
            bulk['y0'] = c_send(0, p, 1)
            bulk['z2'] = c_send(1, p, 2)
            bulk['z4a'] = c_send(2, p, 4, QR[0])
            scores_rows(2 * p)
            scores_rows(2 * p + 1)
        elif it == 0:
            bulk['zx', 1] = z_x(1)
            bulk['z4b'] = c_send(3, p, 4, QR[1])
            for v in range(2):
                for h in range(2):
                    bulk['zp', v, h].wait_recv()
            scores_cols(2 * dp[1])
            scores_cols(2 * dp[1] + 1)
            bulk['y0'].wait_recv()
            bulk['d1'] = c_partner(1)
            bulk['z2'].wait_recv()
            bulk['d2'] = c_partner(2)
            bulk['y2'] = c_send(6, pp[2], 1)
        elif it == 1 and along_data:
            bulk['zx', 2] = z_x(2)
            bulk['z6a'] = c_send(4, p, 6, QR[0])
            scores_rows(2 * pp[1] + half)
            scores_rows(2 * pp[2] + half)
        elif it == 1:
            bulk['zx', 3] = z_x(3)
            bulk['z6b'] = c_send(5, p, 6, QR[1])
            bulk['z4a'].wait_recv()
            bulk['z4b'].wait_recv()
            bulk['d4'] = c_partner(4)
            bulk['y4'] = c_send(7, pp[4], 1)
            bulk['d1'].wait_recv()
            scores_rows(2 * pp[1] + other)
            bulk['d2'].wait_recv()
            scores_rows(2 * pp[2] + other)
            bulk['y2'].wait_recv()
            bulk['d3'] = c_partner(3)
            scores_rows(2 * pp[4] + half)
        elif it == 2 and along_data:
            bulk['z6a'].wait_recv()
            bulk['z6b'].wait_recv()
            bulk['d6'] = c_partner(6)
            bulk['y6'] = c_send(8, pp[6], 1)
            for i in range(4):
                bulk['zx', i].wait_recv()
                bulk['zf', i] = z_partner(8 + i, i // 2, 2 * dp[2] + i % 2)
            scores_rows(2 * pp[3] + half)
            scores_rows(2 * pp[6] + half)
        elif it == 2:
            bulk['y4'].wait_recv()
            bulk['d5'] = c_partner(5)
            scores_cols(2 * dp[2])
            scores_cols(2 * dp[2] + 1)
            for j in (3, 4):
                bulk['d%d' % j].wait_recv()
                scores_rows(2 * pp[j] + other)
            bulk['y6'].wait_recv()
            bulk['d7'] = c_partner(7)
            scores_rows(2 * pp[5] + half)
            scores_rows(2 * pp[7] + half)
        else:
            for i in range(4):
                bulk['zf', i].wait_recv()
            scores_cols(2 * dp[3])
            scores_cols(2 * dp[3] + 1)
            for j in (6, 5, 7):
                bulk['d%d' % j].wait_recv()
                scores_rows(2 * pp[j] + other)

    for it in range(ITERS):
        last = it == ITERS - 1
        for i in range(8):
            ctx[it, i:i + 1] = crow[i]
        cps = [send(ctx.at[it], crx.at[it, j], cs.at[it, j], cr.at[it, j], 0, j) for j in range(1, nd)]
        background(it, True)
        ctot = ctx[it]
        for j, cp in zip(range(1, nd), cps):
            cp.wait_recv()
            ctot = ctot + crx[it, j]
        vt = 1.0 / (total_protos * ctot)
        if last:
            vvec[p] = vt
            vcps = [send(vvec.at[p], vvec.at[p], vs.at[j], vr.at[j], j, 0) for j in range(1, np_)]
        for v in range(2):
            for i in range(4):
                vrep[v, i * L:(i + 1) * L] = jnp.broadcast_to(row_to_col(eye, vt[4 * v + i:4 * v + i + 1]), (L, L))
        for v in range(2):
            racc = [jnp.zeros((8, L), F32) for _ in range(4)]
            tacc = [jnp.zeros((8, L), F32) for _ in range(4)]
            for ck in range(B // CH):
                rows = pl.ds(ck * CH, CH)
                w = vrep[v, rows]
                for j in range(4):
                    lanes = slice(j * L, (j + 1) * L)
                    m = A[v, rows, lanes] * w
                    racc[j] = racc[j] + jnp.sum(m.reshape(CH // 8, 8, L), axis=0)
                    if last:
                        mt = m * T[1 - v, rows, lanes]
                        tacc[j] = tacc[j] + jnp.sum(mt.reshape(CH // 8, 8, L), axis=0)
            for j in range(4):
                rtx[it, 4 * v + j:4 * v + j + 1] = jnp.sum(racc[j], axis=0, keepdims=True)
                if last:
                    rtx[it, 8 + 4 * v + j:8 + 4 * v + j + 1] = jnp.sum(tacc[j], axis=0, keepdims=True)
        if it == 0:
            for i in range(8):
                rtx[it, 8 + i:9 + i] = dsum[i]
        nrow = 8 if it == 1 else 16
        cps = [send(rtx.at[it, 0:nrow], rrx.at[it, j, 0:nrow], rs.at[it, j], rr.at[it, j], j, 0) for j in range(1, np_)]
        background(it, False)
        rtot = rtx[it, 0:nrow]
        for j, cp in zip(range(1, np_), cps):
            cp.wait_recv()
            rtot = rtot + rrx[it, j, 0:nrow]
        if it == 0:
            dfull = rtot[8:16]
        u_tile = 1.0 / (total_rows * rtot[0:8])
        if not last:
            for v in range(2):
                cols = []
                for ck in range(B // CH):
                    rows = pl.ds(ck * CH, CH)
                    part = None
                    for j in range(4):
                        m = A[v, rows, j * L:(j + 1) * L] * u_tile[4 * v + j:4 * v + j + 1]
                        part = m if part is None else part + m
                    cols.append(jnp.sum(part, axis=1, keepdims=True))
                finish_cols(v, cols)

    w = total_rows * u_tile
    logd = jnp.log(dfull)
    swapped = jnp.concatenate([logd[4:8], logd[0:4]], axis=0)
    terms = w * rtot[8:16] * LN2 - (w * rtot[0:8]) * swapped
    tot = jnp.sum(jnp.sum(terms, axis=1, keepdims=True), axis=0, keepdims=True)
    rowv[d, 0:8] = w
    rowv[d, 8:16] = 1.0 / dfull
    rowv[d, 16:24] = jnp.broadcast_to(tot, (8, L))
    ucps = [send(rowv.at[d], rowv.at[d], us.at[j], ur.at[j], 0, j) for j in range(1, nd)]
    background(ITERS, True)
    for cp in ucps + vcps:
        cp.wait_recv()
    for cp in pend:
        cp.wait_send()


def grads_kernel(np_, nd, zall, call, E, ET, rowv, vvec, vrep, q1, q2, loss, g1, g2, gp,
                 H, ucol, qbuf, sem):
    p = lax.axis_index('proto')
    d = lax.axis_index('data')
    total_rows = nd * B
    inv_scale = 1.0 / (2 * total_rows * TEMP_TAU)
    eye = eye_mask()
    lsum = rowv[0, 16:17, 0:1]
    for k in range(1, nd):
        lsum = lsum + rowv[k, 16:17, 0:1]
    loss[...] = lsum * (-1.0 / (2 * total_rows))

    for i in range(16):
        ucol[i // 4, (i % 4) * L:(i % 4 + 1) * L] = jnp.broadcast_to(
            row_to_col(eye, rowv[d, i:i + 1]) * inv_scale, (L, L))

    vt = vvec[p]
    out = []
    for h in range(2):
        for ck in range(B // CH):
            rows = pl.ds(ck * CH, CH)
            for j in range(2):
                lanes = slice(j * L, (j + 1) * L)
                for v in range(2):
                    e = E[v, 2 * p + h, rows, lanes]
                    vrow = vt[4 * v + 2 * h + j:4 * v + 2 * h + j + 1] * (1.0 / inv_scale)
                    qbuf[v, rows, h * HB + j * L:h * HB + (j + 1) * L] = (e * e) * vrow * ucol[v, rows]
    out = [pltpu.make_async_copy(qbuf.at[0], q1, sem.at[0]), pltpu.make_async_copy(qbuf.at[1], q2, sem.at[1])]
    for cp in out:
        cp.start()

    def form_rows(hb, slot):
        vq = vvec[hb // 2]
        par = lax.rem(hb, 2) == 0
        vl = [jnp.where(par, vq[4 * (i // 2) + i % 2:4 * (i // 2) + i % 2 + 1],
                        vq[4 * (i // 2) + 2 + i % 2:4 * (i // 2) + 3 + i % 2]) for i in range(4)]
        for ck in range(B // CH):
            rows = pl.ds(ck * CH, CH)
            for j in range(2):
                lanes = slice(j * L, (j + 1) * L)
                e1 = E[0, hb, rows, lanes]
                e2 = E[1, hb, rows, lanes]
                a1 = (e1 * e1) * vl[j] * ucol[0, rows]
                a2 = (e2 * e2) * vl[2 + j] * ucol[1, rows]
                H[slot, 0, rows, lanes] = (e1 * ucol[2, rows] - a2).astype(BF16)
                H[slot, 1, rows, lanes] = (e2 * ucol[3, rows] - a1).astype(BF16)

    g1[...] = jnp.zeros_like(g1)
    g2[...] = jnp.zeros_like(g2)
    gp[...] = jnp.zeros_like(gp)
    n_hb = 2 * np_
    form_rows(0, 0)

    def row_step(i, carry):
        for s in range(2):
            hb = 2 * i + s
            cb = call[hb]
            g1[...] += jnp.dot(H[s, 0], cb, preferred_element_type=F32)
            g2[...] += jnp.dot(H[s, 1], cb, preferred_element_type=F32)
            form_rows(lax.rem(hb + 1, n_hb), 1 - s)
        return carry

    lax.fori_loop(0, np_, row_step, 0)

    def form_cols(nb, slot):
        rv = rowv[nb // 2, 0:16] * inv_scale
        par = lax.rem(nb, 2) == 0
        rl = [jnp.where(par, rv[4 * (i // 2) + i % 2:4 * (i // 2) + i % 2 + 1],
                        rv[4 * (i // 2) + 2 + i % 2:4 * (i // 2) + 3 + i % 2]) for i in range(8)]
        for ck in range(B // CH):
            rows = pl.ds(ck * CH, CH)
            for j in range(2):
                lanes = slice(j * L, (j + 1) * L)
                e1 = ET[0, nb, rows, lanes]
                e2 = ET[1, nb, rows, lanes]
                a1 = (e1 * e1) * rl[j] * vrep[0, rows]
                a2 = (e2 * e2) * rl[2 + j] * vrep[1, rows]
                H[slot, 0, rows, lanes] = (e1 * rl[4 + j] - a2).astype(BF16)
                H[slot, 1, rows, lanes] = (e2 * rl[6 + j] - a1).astype(BF16)

    n_nb = 2 * nd
    form_cols(0, 0)

    def col_step(i, carry):
        for s in range(2):
            nb = 2 * i + s
            gp[...] += (jnp.dot(H[s, 0], zall[0, nb], preferred_element_type=F32)
                        + jnp.dot(H[s, 1], zall[1, nb], preferred_element_type=F32))
            form_cols(lax.rem(nb + 1, n_nb), 1 - s)
        return carry

    lax.fori_loop(0, nd, col_step, 0)
    for cp in out:
        cp.wait()


def solution(mesh):
    np_ = mesh.shape['proto']
    nd = mesh.shape['data']
    VM = pl.BlockSpec(memory_space=pltpu.VMEM)
    HBM = pl.BlockSpec(memory_space=pltpu.HBM)
    ANY = pl.BlockSpec(memory_space=pl.ANY)
    DMA = pltpu.SemaphoreType.DMA

    def local_step(emb_one, emb_two, protos):
        dim = protos.shape[1]
        mid = pl.pallas_call(
            functools.partial(sinkhorn_kernel, np_, nd),
            out_shape=(jax.ShapeDtypeStruct((2, 2 * nd, HB, dim), BF16),
                       jax.ShapeDtypeStruct((2 * np_, HB, dim), BF16),
                       jax.ShapeDtypeStruct((2, 2 * np_, B, HB), F32),
                       jax.ShapeDtypeStruct((2, 2 * nd, B, HB), F32),
                       jax.ShapeDtypeStruct((nd, 24, L), F32), jax.ShapeDtypeStruct((np_, 8, L), F32),
                       jax.ShapeDtypeStruct((2, B, L), F32)),
            in_specs=[HBM] * 3, out_specs=(VM,) * 7,
            scratch_shapes=[
                pltpu.VMEM((2, B, B), F32), pltpu.VMEM((2, B, B), F32),
                pltpu.VMEM((ITERS, 8, L), F32), pltpu.VMEM((ITERS, nd, 8, L), F32),
                pltpu.VMEM((ITERS, 16, L), F32), pltpu.VMEM((ITERS, np_, 16, L), F32),
                DMA((6,)), DMA((ITERS, nd)), DMA((ITERS, nd)), DMA((ITERS, np_)), DMA((ITERS, np_)),
                DMA((np_,)), DMA((np_,)), DMA((nd,)), DMA((nd,)),
                DMA((12,)), DMA((12,)), DMA((9,)), DMA((9,)), DMA((np_,)), DMA((np_,))],
            compiler_params=pltpu.CompilerParams(collective_id=0, has_side_effects=True, vmem_limit_bytes=12 << 20),
            name='sinkhorn',
        )(*[pltpu.with_memory_space_constraint(a, pltpu.HBM) for a in (emb_one, emb_two, protos)])
        q1, q2, loss, g1, g2, gp = pl.pallas_call(
            functools.partial(grads_kernel, np_, nd),
            out_shape=(jax.ShapeDtypeStruct((B, B), F32), jax.ShapeDtypeStruct((B, B), F32),
                       jax.ShapeDtypeStruct((1, 1), F32),
                       jax.ShapeDtypeStruct((B, dim), F32), jax.ShapeDtypeStruct((B, dim), F32),
                       jax.ShapeDtypeStruct((B, dim), F32)),
            in_specs=[VM] * 7, out_specs=(ANY, ANY, VM, VM, VM, VM),
            scratch_shapes=[pltpu.VMEM((2, 2, B, HB), BF16), pltpu.VMEM((4, B, L), F32),
                            pltpu.VMEM((2, B, B), F32), DMA((2,))],
            compiler_params=pltpu.CompilerParams(vmem_limit_bytes=12 << 20),
            name='grads',
        )(*mid)
        return q1, q2, loss.reshape(()), g1, g2, gp

    return jax.shard_map(
        local_step, mesh=mesh,
        in_specs=(P('data', None), P('data', None), P('proto', None)),
        out_specs=(P('data', 'proto'), P('data', 'proto'), P(), P('data', None), P('data', None), P('proto', None)),
        check_vma=False)
```

time: 57.7 us -> 47.6 us (0.82)
  Pallas kernels: 56.9 us -> 46.4 us
    pallas_call x1, Pallas kernels: 17.5 us -> 10.4 us  [local_step(): pl.pallas_call(functools.partial(grads_kernel, np_, nd), out_shape=(jax.S...]
    pallas_call x1, Pallas kernels: 39.4 us -> 36 us  [local_step(): pl.pallas_call(functools.partial(sinkhorn_kernel, np_, nd), out_shape=(ja...]
where the time goes in v2:
time: 47.6 us; the launch traced here: 47 us
  Pallas kernels  46.4 us (97%)
  between operations  0.64 us (1%)
    pallas_call x1, Pallas kernels, local_step(): pl.pallas_call(functools.partial(sinkhorn_kernel, np_, nd), out_shape=(ja...  36 us
    pallas_call x1, Pallas kernels, local_step(): pl.pallas_call(functools.partial(grads_kernel, np_, nd), out_shape=(jax.S...  10.4 us

profile of v2, /device:TPU:1, one launch (start us, length us, event | category | flops | bytes accessed | tf_op | source)
XLA Modules:
  0.0 47.0 jit_solution(2714953195506098878)
XLA Ops:
  0.6 36.0 %sinkhorn.1 = (bf16[2,8,256,256]{3,2,1,0:T(8,128)(2,1)S(1)}, bf16[16,256,256]{2,1,0:T(8,128)(2,1)S(1)}, f32[2,16,512,256]{3,2,1,0:T(8,128)S(1)}, f32[2,8,512,256...) custom-call(bf16[512,256]{1,0:T(8,128)(2,1)} %z1.1, ...), custom_call_target="tpu_custom_call" | custom-call | tf_op jit(solution)/shard_map/sinkhorn/pallas_call | solution.py:408
  36.6 10.4 %grads.1 = (f32[512,512]{1,0:T(8,128)}, f32[512,512]{1,0:T(8,128)}, f32[1,1]{1,0:T(1,128)}, f32[512,256]{1,0:T(8,128)}, f32[512,256]{1,0:T(8,128)}, /*index=5*/f32[512,256]{1,0:T(8,128)}) custom-call(bf16[2,8,256,256]{3,2,1,0:T(8,128)(2,1)S(1)} %get-tuple-element.19.zall, bf16[16,256,256]{2,1,0:T(8,128)(2,1)S(1)} %get-tuple-element.20.call, ...), custom_call_target="tpu_custom_call" | custom-call | tf_op jit(solution)/shard_map/grads/pallas_call | solution.py:427

commit v3 on v2

v3 whole, which is shorter than its diff:
```python
import functools
import math

import jax
import jax.numpy as jnp
from jax import lax
from jax.experimental import pallas as pl
from jax.experimental.pallas import tpu as pltpu
from jax.sharding import PartitionSpec as P

TEMP_TAU = 0.1
ITERS = 3
F32, BF16 = jnp.float32, jnp.bfloat16
LOG2E_TAU = math.log2(math.e) / TEMP_TAU
LN2 = math.log(2.0)
B = 512
HB = 256
L = 128
CH = 64
EARLY = 4
RC = 16
NT = (((1,), (1,)), ((), ()))


def eye_mask():
    return lax.broadcasted_iota(jnp.int32, (L, L), 0) == lax.broadcasted_iota(jnp.int32, (L, L), 1)


def col_to_row(eye, col):
    return jnp.sum(jnp.where(eye, col, 0.0), axis=0, keepdims=True)


def row_to_col(eye, row):
    return jnp.sum(jnp.where(eye, row, 0.0), axis=1, keepdims=True)


def xor(a, k):
    out = a
    for bit in (1, 2, 4):
        if k & bit:
            out = out + bit - 2 * bit * lax.rem(out // bit, 2)
    return out


def xor2(a, b):
    out = 0
    for bit in (1, 2, 4):
        out = out + bit * lax.rem(lax.rem(a // bit, 2) + lax.rem(b // bit, 2), 2)
    return out


def form_rows(E, vvec, ucol, H, q):
    vq = vvec[q]
    for ck in range(B // RC):
        rows = pl.ds(ck * RC, RC)
        u1, u2 = ucol[0, rows], ucol[1, rows]
        for j in range(4):
            lanes = slice((j % 2) * L, (j % 2 + 1) * L)
            p1 = E[0, 2 * q + j // 2, rows, lanes]
            p2 = E[1, 2 * q + j // 2, rows, lanes]
            a1 = (p1 * p1) * u1 * vq[j:j + 1]
            a2 = (p2 * p2) * u2 * vq[4 + j:5 + j]
            H[0, rows, j * L:(j + 1) * L] = (p1 - a2).astype(BF16)
            H[1, rows, j * L:(j + 1) * L] = (p2 - a1).astype(BF16)


def dz_blocks(E, vvec, ucol, H, call, G, p, lo, hi, first):
    form_rows(E, vvec, ucol, H.at[0], xor2(p, lo))
    if first:
        G[...] = jnp.zeros_like(G)

    def two(i, carry):
        for s in range(2):
            j = lo + 2 * i + s
            q = xor2(p, j)
            for v in range(2):
                G[v] += times_block(H.at[s], v, call, q)
            form_rows(E, vvec, ucol, H.at[1 - s], xor2(p, lax.rem(j + 1, 8)))
        return carry

    lax.fori_loop(0, (hi - lo) // 2, two, 0)


def times_block(H, v, call, q):
    return jnp.dot(H[v], call[pl.ds(2 * q, 2)].reshape(B, -1), preferred_element_type=F32)


def sinkhorn_kernel(np_, nd, z1, z2, c, zall, call, E, ET, rowv, vvec, vrep, ucol, G,
                    T, A, H, dall, ctx, crx, rtx, rrx,
                    lsem, cs, cr, rs, rr, vs, vr, us, ur, zs, zr, gs, gr, ds_, dr_):
    p = lax.axis_index('proto')
    d = lax.axis_index('data')
    total_rows = nd * B
    total_protos = np_ * B
    inv_scale = 1.0 / (2 * total_rows * TEMP_TAU)
    half = lax.rem(d, 2)
    other = 1 - half

    loads = [pltpu.make_async_copy(z1.at[h * HB:(h + 1) * HB], zall.at[0, 2 * d + h], lsem.at[h]) for h in range(2)]
    loads += [pltpu.make_async_copy(z2.at[h * HB:(h + 1) * HB], zall.at[1, 2 * d + h], lsem.at[2 + h]) for h in range(2)]
    loads += [pltpu.make_async_copy(c.at[h * HB:(h + 1) * HB], call.at[2 * p + h], lsem.at[4 + h]) for h in range(2)]
    for cp in loads:
        cp.start()

    dp = [xor(d, j) for j in range(nd)]
    pp = [xor(p, j) for j in range(np_)]

    bar = pltpu.get_barrier_semaphore()
    for j in range(1, nd):
        pl.semaphore_signal(bar, inc=1, device_id={'proto': p, 'data': dp[j]})
    for j in range(1, np_):
        pl.semaphore_signal(bar, inc=1, device_id={'proto': pp[j], 'data': d})

    for cp in loads:
        cp.wait()

    pend = []

    def send(src, dst, ss, rs_, pj, dj):
        cp = pltpu.make_async_remote_copy(src, dst, ss, rs_, device_id={'proto': pp[pj], 'data': dp[dj]})
        cp.start()
        pend.append(cp)
        return cp

    def z_x(i):
        ref = zall.at[i // 2, 2 * d + i % 2]
        return send(ref, ref, zs.at[i], zr.at[i], 0, 2)

    def z_partner(slot, v, nb):
        ref = zall.at[v, nb]
        return send(ref, ref, zs.at[slot], zr.at[slot], 0, 1)

    def c_send(slot, q, pj):
        ref = call.at[2 * q + half]
        return send(ref, ref, gs.at[slot], gr.at[slot], pj, 0)

    def c_partner(j):
        ref = call.at[2 * pp[j] + half]
        return send(ref, ref, ds_.at[j], dr_.at[j], 0, 1)

    def own_images(v):
        return zall[v, pl.ds(2 * d, 2)].reshape(B, -1)

    def own_protos():
        return call[pl.ds(2 * p, 2)].reshape(B, -1)

    def scores_rows(hb):
        for v in range(2):
            s = lax.dot_general(own_images(v), call[hb], NT, preferred_element_type=F32)
            for j in range(2):
                lanes = slice(j * L, (j + 1) * L)
                E[v, hb, :, lanes] = jnp.exp2(s[:, lanes] * LOG2E_TAU) * ucol[2 + v]

    def scores_cols(nb):
        for v in range(2):
            s = lax.dot_general(own_protos(), zall[v, nb], NT, preferred_element_type=F32)
            for j in range(2):
                lanes = slice(j * L, (j + 1) * L)
                row = pl.ds(4 * v + 2 * lax.rem(nb, 2) + j, 1)
                ET[v, nb, :, lanes] = jnp.exp2(s[:, lanes] * LOG2E_TAU) * dall[nb // 2, row]

    eye = eye_mask()

    crow = [None] * 8
    dsum = [None] * 8
    for v in range(2):
        dacc = [None] * 4
        for h in range(2):
            part = None
            for h2 in range(2):
                s = lax.dot_general(call[2 * p + h], zall[v, 2 * d + h2], NT, preferred_element_type=F32)
                e = jnp.exp2(s * LOG2E_TAU)
                A[v, h * HB:(h + 1) * HB, h2 * HB:(h2 + 1) * HB] = e
                a = e * e
                for j in range(2):
                    lanes = slice(j * L, (j + 1) * L)
                    ds = jnp.sum(e[:, lanes].reshape(HB // 8, 8, L), axis=0)
                    k = 2 * h2 + j
                    dacc[k] = ds if dacc[k] is None else dacc[k] + ds
                    part = a[:, lanes] if part is None else part + a[:, lanes]
            col = jnp.sum(part, axis=1, keepdims=True)
            for i in range(2):
                crow[4 * v + 2 * h + i] = col_to_row(eye, col[i * L:(i + 1) * L])
        for j in range(4):
            dsum[4 * v + j] = jnp.sum(dacc[j], axis=0, keepdims=True)

    pl.semaphore_wait(bar, nd - 1 + np_ - 1)

    bulk = {}

    def background(it, along_data):
        if it == 0 and along_data:
            bulk['y0'] = c_send(0, p, 1)
            bulk['z2'] = c_send(1, p, 2)
            bulk['zx', 0] = z_x(0)
            for v in range(2):
                for h in range(2):
                    bulk['zp', v, h] = z_partner(4 + 2 * v + h, v, 2 * d + h)
            for v in range(2):
                for ck in range(B // CH):
                    rows = pl.ds(ck * CH, CH)
                    e = A[v, rows]
                    for h in range(2):
                        ET[v, 2 * d + h, rows] = e[:, h * HB:(h + 1) * HB]
                    A[v, rows] = e * e
            for v in range(2):
                T[v] = lax.dot_general(own_protos(), own_images(v), NT, preferred_element_type=F32) * LOG2E_TAU
        elif it == 0:
            bulk['z4'] = c_send(2, p, 4)
            bulk['zx', 1] = z_x(1)
            bulk['y0'].wait_recv()
            bulk['d1'] = c_partner(1)
            bulk['z2'].wait_recv()
            bulk['y2'] = c_send(4, pp[2], 1)
            bulk['d2'] = c_partner(2)
        elif it == 1 and along_data:
            bulk['zx', 2] = z_x(2)
            for i in range(8):
                ucol[2 + i // 4, (i % 4) * L:(i % 4 + 1) * L] = jnp.broadcast_to(
                    row_to_col(eye, dscale[i:i + 1]), (L, L))
            scores_rows(2 * p)
            scores_rows(2 * p + 1)
            scores_rows(2 * pp[1] + half)
        elif it == 1:
            bulk['z6'] = c_send(3, p, 6)
            bulk['zx', 3] = z_x(3)
            bulk['z4'].wait_recv()
            bulk['y4'] = c_send(5, pp[4], 1)
            bulk['d4'] = c_partner(4)
            bulk['y2'].wait_recv()
            bulk['d3'] = c_partner(3)
            scores_rows(2 * pp[2] + half)
            for j in (1, 2):
                bulk['d%d' % j].wait_recv()
                scores_rows(2 * pp[j] + other)
            for v in range(2):
                for h in range(2):
                    bulk['zp', v, h].wait_recv()
            scores_cols(2 * dp[1])
            scores_cols(2 * dp[1] + 1)
            scores_rows(2 * pp[4] + half)
            scores_rows(2 * pp[3] + half)
            for v in range(2):
                for h in range(2):
                    for j in range(2):
                        lanes = slice(j * L, (j + 1) * L)
                        k = 4 * v + 2 * h + j
                        ET[v, 2 * d + h, :, lanes] = ET[v, 2 * d + h, :, lanes] * dscale[k:k + 1]
        elif it == 2 and along_data:
            for j in (4, 3):
                bulk['d%d' % j].wait_recv()
                scores_rows(2 * pp[j] + other)
            for i in range(4):
                bulk['zx', i].wait_recv()
                bulk['zf', i] = z_partner(8 + i, i // 2, 2 * dp[2] + i % 2)
            scores_cols(2 * dp[2])
            scores_cols(2 * dp[2] + 1)
        elif it == 2:
            bulk['z6'].wait_recv()
            bulk['y6'] = c_send(6, pp[6], 1)
            bulk['d6'] = c_partner(6)
            bulk['y4'].wait_recv()
            bulk['d5'] = c_partner(5)
            for i in range(4):
                bulk['zf', i].wait_recv()
            scores_cols(2 * dp[3])
            scores_cols(2 * dp[3] + 1)
            for j in (6, 5):
                scores_rows(2 * pp[j] + half)
                bulk['d%d' % j].wait_recv()
                scores_rows(2 * pp[j] + other)
        else:
            for i in range(8):
                ucol[i // 4, (i % 4) * L:(i % 4 + 1) * L] = jnp.broadcast_to(
                    row_to_col(eye, useg[i:i + 1]), (L, L))
            for cp in vcps:
                cp.wait_recv()
            dz_blocks(E, vvec, ucol, H, call, G, p, 0, EARLY, True)
            bulk['y6'].wait_recv()
            bulk['d7'] = c_partner(7)
            scores_rows(2 * pp[7] + half)
            bulk['d7'].wait_recv()
            scores_rows(2 * pp[7] + other)

    for it in range(ITERS):
        last = it == ITERS - 1
        for i in range(8):
            ctx[it, i:i + 1] = crow[i]
        nc = 8
        if it == 1:
            nc = 16
            ctx[it, 8:16] = dscale
        cps = [send(ctx.at[it, 0:nc], crx.at[it, j, 0:nc], cs.at[it, j], cr.at[it, j], 0, j) for j in range(1, nd)]
        background(it, True)
        ctot = ctx[it, 0:8]
        for j, cp in zip(range(1, nd), cps):
            cp.wait_recv()
            ctot = ctot + crx[it, j, 0:8]
        if it == 1:
            dall[d] = dscale
            for j in range(1, nd):
                dall[dp[j]] = crx[it, j, 8:16]
        vt = 1.0 / (total_protos * ctot)
        if last:
            vvec[p] = vt
            vcps = [send(vvec.at[p], vvec.at[p], vs.at[j], vr.at[j], j, 0) for j in range(1, np_)]
        for v in range(2):
            for i in range(4):
                vrep[v, i * L:(i + 1) * L] = jnp.broadcast_to(row_to_col(eye, vt[4 * v + i:4 * v + i + 1]), (L, L))
        for v in range(2):
            racc = [jnp.zeros((8, L), F32) for _ in range(4)]
            tacc = [jnp.zeros((8, L), F32) for _ in range(4)]
            for ck in range(B // CH):
                rows = pl.ds(ck * CH, CH)
                wv = vrep[v, rows]
                for j in range(4):
                    lanes = slice(j * L, (j + 1) * L)
                    m = A[v, rows, lanes] * wv
                    racc[j] = racc[j] + jnp.sum(m.reshape(CH // 8, 8, L), axis=0)
                    if last:
                        mt = m * T[1 - v, rows, lanes]
                        tacc[j] = tacc[j] + jnp.sum(mt.reshape(CH // 8, 8, L), axis=0)
            for j in range(4):
                rtx[it, 4 * v + j:4 * v + j + 1] = jnp.sum(racc[j], axis=0, keepdims=True)
                if last:
                    rtx[it, 8 + 4 * v + j:8 + 4 * v + j + 1] = jnp.sum(tacc[j], axis=0, keepdims=True)
        if it == 0:
            for i in range(8):
                rtx[it, 8 + i:9 + i] = dsum[i]
        nrow = 8 if it == 1 else 16
        cps = [send(rtx.at[it, 0:nrow], rrx.at[it, j, 0:nrow], rs.at[it, j], rr.at[it, j], j, 0) for j in range(1, np_)]
        background(it, False)
        rtot = rtx[it, 0:nrow]
        for j, cp in zip(range(1, np_), cps):
            cp.wait_recv()
            rtot = rtot + rrx[it, j, 0:nrow]
        if it == 0:
            dfull = rtot[8:16]
            dscale = inv_scale / dfull
        u_tile = 1.0 / (total_rows * rtot[0:8])
        if not last:
            for v in range(2):
                cols = []
                for ck in range(B // CH):
                    rows = pl.ds(ck * CH, CH)
                    part = None
                    for j in range(4):
                        m = A[v, rows, j * L:(j + 1) * L] * u_tile[4 * v + j:4 * v + j + 1]
                        part = m if part is None else part + m
                    cols.append(jnp.sum(part, axis=1, keepdims=True))
                per = L // CH
                for i in range(4):
                    crow[4 * v + i] = col_to_row(eye, jnp.concatenate(cols[per * i:per * (i + 1)], axis=0))

    w = total_rows * u_tile
    logd = jnp.log(dfull)
    swapped = jnp.concatenate([logd[4:8], logd[0:4]], axis=0)
    terms = w * rtot[8:16] * LN2 - (w * rtot[0:8]) * swapped
    tot = jnp.sum(jnp.sum(terms, axis=1, keepdims=True), axis=0, keepdims=True)
    useg = w * inv_scale / (dscale * dscale)
    rowv[d, 0:8] = useg
    rowv[d, 8:16] = jnp.broadcast_to(tot, (8, L))
    ucps = [send(rowv.at[d], rowv.at[d], us.at[j], ur.at[j], 0, j) for j in range(1, nd)]
    background(ITERS, True)
    for cp in ucps:
        cp.wait_recv()
    for cp in pend:
        cp.wait_send()


def grads_kernel(np_, nd, zall, call, E, ET, rowv, vvec, vrep, ucol, G, q1, q2, loss, g1, g2, gp,
                 H, qbuf, gbuf, gsum, sem):
    p = lax.axis_index('proto')
    d = lax.axis_index('data')
    total_rows = nd * B
    scale = 2 * total_rows * TEMP_TAU
    inv_scale = 1.0 / scale
    lsum = rowv[0, 8:9, 0:1]
    for k in range(1, nd):
        lsum = lsum + rowv[k, 8:9, 0:1]
    loss[...] = lsum * (-1.0 / (2 * total_rows))

    vt = vvec[p] * scale

    def codes(ck, carry):
        rows = pl.ds(pl.multiple_of(ck * CH, CH), CH)
        for v in range(2):
            uv = ucol[v, rows]
            for j in range(4):
                e = E[v, 2 * p + j // 2, rows, (j % 2) * L:(j % 2 + 1) * L]
                qbuf[v, rows, j * L:(j + 1) * L] = (e * e) * uv * vt[4 * v + j:4 * v + j + 1]
        return carry

    lax.fori_loop(0, B // CH, codes, 0)
    out = [pltpu.make_async_copy(qbuf.at[0], q1, sem.at[0]), pltpu.make_async_copy(qbuf.at[1], q2, sem.at[1])]
    for cp in out:
        cp.start()

    gbuf[0:2] = G[...]
    dz_blocks(E, vvec, ucol, H, call, gbuf, p, EARLY, np_, False)
    gout = [pltpu.make_async_copy(gbuf.at[0], g1, sem.at[2]), pltpu.make_async_copy(gbuf.at[1], g2, sem.at[3])]
    for cp in gout:
        cp.start()

    def form_cols(Hs, k):
        rv = rowv[k, 0:8]
        for ck in range(B // RC):
            rows = pl.ds(ck * RC, RC)
            v1, v2 = vrep[0, rows], vrep[1, rows]
            for j in range(4):
                lanes = slice((j % 2) * L, (j % 2 + 1) * L)
                p1 = ET[0, 2 * k + j // 2, rows, lanes]
                p2 = ET[1, 2 * k + j // 2, rows, lanes]
                a1 = (p1 * p1) * rv[j:j + 1] * v1
                a2 = (p2 * p2) * rv[4 + j:5 + j] * v2
                Hs[0, rows, j * L:(j + 1) * L] = (p1 - a2).astype(BF16)
                Hs[1, rows, j * L:(j + 1) * L] = (p2 - a1).astype(BF16)

    form_cols(H.at[0], 0)
    gsum[...] = jnp.zeros_like(gsum)

    def two(i, carry):
        for s in range(2):
            k = 2 * i + s
            t = [jnp.dot(H[s, v], zall[v, pl.ds(2 * k, 2)].reshape(B, -1), preferred_element_type=F32) for v in range(2)]
            gsum[...] += t[0] + t[1]
            form_cols(H.at[1 - s], lax.rem(k + 1, nd))
        return carry

    lax.fori_loop(0, nd // 2, two, 0)
    gout.append(pltpu.make_async_copy(gsum, gp, sem.at[4]))
    gout[-1].start()
    for cp in out + gout:
        cp.wait()


def solution(mesh):
    np_ = mesh.shape['proto']
    nd = mesh.shape['data']
    VM = pl.BlockSpec(memory_space=pltpu.VMEM)
    HBM = pl.BlockSpec(memory_space=pltpu.HBM)
    ANY = pl.BlockSpec(memory_space=pl.ANY)
    DMA = pltpu.SemaphoreType.DMA

    def local_step(emb_one, emb_two, protos):
        dim = protos.shape[1]
        sds = jax.ShapeDtypeStruct
        mid = pl.pallas_call(
            functools.partial(sinkhorn_kernel, np_, nd),
            out_shape=(sds((2, 2 * nd, HB, dim), BF16), sds((2 * np_, HB, dim), BF16),
                       sds((2, 2 * np_, B, HB), F32), sds((2, 2 * nd, B, HB), F32),
                       sds((nd, 16, L), F32), sds((np_, 8, L), F32),
                       sds((2, B, L), F32), sds((4, B, L), F32), sds((2, B, dim), F32)),
            in_specs=[HBM] * 3, out_specs=(VM,) * 9,
            scratch_shapes=[
                pltpu.VMEM((2, B, B), F32), pltpu.VMEM((2, B, B), F32), pltpu.VMEM((2, 2, B, B), BF16),
                pltpu.VMEM((nd, 8, L), F32),
                pltpu.VMEM((ITERS, 16, L), F32), pltpu.VMEM((ITERS, nd, 16, L), F32),
                pltpu.VMEM((ITERS, 16, L), F32), pltpu.VMEM((ITERS, np_, 16, L), F32),
                DMA((6,)), DMA((ITERS, nd)), DMA((ITERS, nd)), DMA((ITERS, np_)), DMA((ITERS, np_)),
                DMA((np_,)), DMA((np_,)), DMA((nd,)), DMA((nd,)),
                DMA((12,)), DMA((12,)), DMA((7,)), DMA((7,)), DMA((np_,)), DMA((np_,))],
            compiler_params=pltpu.CompilerParams(collective_id=0, has_side_effects=True, vmem_limit_bytes=10 << 20),
            name='sinkhorn',
        )(*[pltpu.with_memory_space_constraint(a, pltpu.HBM) for a in (emb_one, emb_two, protos)])
        q1, q2, loss, g1, g2, gp = pl.pallas_call(
            functools.partial(grads_kernel, np_, nd),
            out_shape=(sds((B, B), F32), sds((B, B), F32), sds((1, 1), F32),
                       sds((B, dim), F32), sds((B, dim), F32), sds((B, dim), F32)),
            in_specs=[VM] * 9, out_specs=(ANY, ANY, VM, ANY, ANY, ANY),
            scratch_shapes=[pltpu.VMEM((2, 2, B, B), BF16), pltpu.VMEM((2, B, B), F32),
                            pltpu.VMEM((2, B, dim), F32), pltpu.VMEM((B, dim), F32), DMA((5,))],
            compiler_params=pltpu.CompilerParams(vmem_limit_bytes=17 << 20),
            name='grads',
        )(*mid)
        return q1, q2, loss.reshape(()), g1, g2, gp

    return jax.shard_map(
        local_step, mesh=mesh,
        in_specs=(P('data', None), P('data', None), P('proto', None)),
        out_specs=(P('data', 'proto'), P('data', 'proto'), P(), P('data', None), P('data', None), P('proto', None)),
        check_vma=False)
```

time: 47.6 us -> 45.5 us (0.956)
  Pallas kernels: 46.4 us -> 44.5 us
    pallas_call x2, Pallas kernels: 46.4 us -> 44.5 us  [the longest x1 37.5 us: local_step(): pl.pallas_call(functools.partial(sinkhorn_kernel, np_, nd), out_shape=(sd...]
where the time goes in v3:
time: 45.5 us; the launch traced here: 45.3 us
  Pallas kernels  44.5 us (98%)
  between operations  0.8 us (2%)
    pallas_call x1, Pallas kernels, local_step(): pl.pallas_call(functools.partial(sinkhorn_kernel, np_, nd), out_shape=(sd...  37.5 us
    pallas_call x1, Pallas kernels, local_step(): pl.pallas_call(functools.partial(grads_kernel, np_, nd), out_shape=(sds((...  6.99 us

profile of v3, /device:TPU:1, one launch (start us, length us, event | category | flops | bytes accessed | tf_op | source)
XLA Modules:
  0.0 45.3 jit_solution(9683272115125877327)
XLA Ops:
  0.6 37.5 %sinkhorn.1 = (bf16[2,8,256,256]{3,2,1,0:T(8,128)(2,1)S(1)}, bf16[16,256,256]{2,1,0:T(8,128)(2,1)S(1)}, f32[2,16,512,256]{3,2,1,0:T(8,128)S(1)}, f32[2,8,512,256...) custom-call(bf16[512,256]{1,0:T(8,128)(2,1)} %z1.1, ...), custom_call_target="tpu_custom_call" | custom-call | tf_op jit(solution)/shard_map/sinkhorn/pallas_call | solution.py:448
  38.2 7.0 %grads.1 = (f32[512,512]{1,0:T(8,128)}, f32[512,512]{1,0:T(8,128)}, f32[1,1]{1,0:T(1,128)}, f32[512,256]{1,0:T(8,128)}, f32[512,256]{1,0:T(8,128)}, /*index=5*/f32[512,256]{1,0:T(8,128)}) custom-call(bf16[2,8,256,256]{3,2,1,0:T(8,128)(2,1)S(1)} %get-tuple-element.21.zall, bf16[16,256,256]{2,1,0:T(8,128)(2,1)S(1)} %get-tuple-element.22.call, ...), custom_call_target="tpu_custom_call" | custom-call | tf_op jit(solution)/shard_map/grads/pallas_call | solution.py:466

commit v4 on v3

--- a/solution.py
+++ b/solution.py
@@ -60,8 +60,8 @@
             p2 = E[1, 2 * q + j // 2, rows, lanes]
             a1 = (p1 * p1) * u1 * vq[j:j + 1]
             a2 = (p2 * p2) * u2 * vq[4 + j:5 + j]
-            H[0, rows, j * L:(j + 1) * L] = (p1 - a2).astype(BF16)
-            H[1, rows, j * L:(j + 1) * L] = (p2 - a1).astype(BF16)
+            H[0, j, rows] = (p1 - a2).astype(BF16)
+            H[1, j, rows] = (p2 - a1).astype(BF16)
 
 
 def dz_blocks(E, vvec, ucol, H, call, G, p, lo, hi, first):
@@ -81,8 +81,12 @@
     lax.fori_loop(0, (hi - lo) // 2, two, 0)
 
 
+def slabs(H, v):
+    return jnp.concatenate([H[v, j] for j in range(4)], axis=1)
+
+
 def times_block(H, v, call, q):
-    return jnp.dot(H[v], call[pl.ds(2 * q, 2)].reshape(B, -1), preferred_element_type=F32)
+    return jnp.dot(slabs(H, v), call[pl.ds(2 * q, 2)].reshape(B, -1), preferred_element_type=F32)
 
 
 def sinkhorn_kernel(np_, nd, z1, z2, c, zall, call, E, ET, rowv, vvec, vrep, ucol, G,
@@ -130,8 +134,10 @@
         ref = zall.at[v, nb]
         return send(ref, ref, zs.at[slot], zr.at[slot], 0, 1)
 
-    def c_send(slot, q, pj):
+    def c_send(slot, q, pj, part=None):
         ref = call.at[2 * q + half]
+        if part is not None:
+            ref = ref.at[part * L:(part + 1) * L]
         return send(ref, ref, gs.at[slot], gr.at[slot], pj, 0)
 
     def c_partner(j):
@@ -191,6 +197,7 @@
     def background(it, along_data):
         if it == 0 and along_data:
             bulk['y0'] = c_send(0, p, 1)
+            bulk['z4', 0] = c_send(2, p, 4, 0)
             bulk['z2'] = c_send(1, p, 2)
             bulk['zx', 0] = z_x(0)
             for v in range(2):
@@ -206,7 +213,6 @@
             for v in range(2):
                 T[v] = lax.dot_general(own_protos(), own_images(v), NT, preferred_element_type=F32) * LOG2E_TAU
         elif it == 0:
-            bulk['z4'] = c_send(2, p, 4)
             bulk['zx', 1] = z_x(1)
             bulk['y0'].wait_recv()
             bulk['d1'] = c_partner(1)
@@ -214,6 +220,8 @@
             bulk['y2'] = c_send(4, pp[2], 1)
             bulk['d2'] = c_partner(2)
         elif it == 1 and along_data:
+            bulk['z4', 1] = c_send(3, p, 4, 1)
+            bulk['z6', 0] = c_send(7, p, 6, 0)
             bulk['zx', 2] = z_x(2)
             for i in range(8):
                 ucol[2 + i // 4, (i % 4) * L:(i % 4 + 1) * L] = jnp.broadcast_to(
@@ -222,9 +230,9 @@
             scores_rows(2 * p + 1)
             scores_rows(2 * pp[1] + half)
         elif it == 1:
-            bulk['z6'] = c_send(3, p, 6)
             bulk['zx', 3] = z_x(3)
-            bulk['z4'].wait_recv()
+            bulk['z4', 0].wait_recv()
+            bulk['z4', 1].wait_recv()
             bulk['y4'] = c_send(5, pp[4], 1)
             bulk['d4'] = c_partner(4)
             bulk['y2'].wait_recv()
@@ -240,6 +248,8 @@
             scores_cols(2 * dp[1] + 1)
             scores_rows(2 * pp[4] + half)
             scores_rows(2 * pp[3] + half)
+            bulk['z6', 0].wait_recv()
+            bulk['y6', 0] = c_send(6, pp[6], 1, 0)
             for v in range(2):
                 for h in range(2):
                     for j in range(2):
@@ -247,6 +257,7 @@
                         k = 4 * v + 2 * h + j
                         ET[v, 2 * d + h, :, lanes] = ET[v, 2 * d + h, :, lanes] * dscale[k:k + 1]
         elif it == 2 and along_data:
+            bulk['z6', 1] = c_send(8, p, 6, 1)
             for j in (4, 3):
                 bulk['d%d' % j].wait_recv()
                 scores_rows(2 * pp[j] + other)
@@ -256,8 +267,8 @@
             scores_cols(2 * dp[2])
             scores_cols(2 * dp[2] + 1)
         elif it == 2:
-            bulk['z6'].wait_recv()
-            bulk['y6'] = c_send(6, pp[6], 1)
+            bulk['z6', 1].wait_recv()
+            bulk['y6', 1] = c_send(9, pp[6], 1, 1)
             bulk['d6'] = c_partner(6)
             bulk['y4'].wait_recv()
             bulk['d5'] = c_partner(5)
@@ -276,7 +287,8 @@
             for cp in vcps:
                 cp.wait_recv()
             dz_blocks(E, vvec, ucol, H, call, G, p, 0, EARLY, True)
-            bulk['y6'].wait_recv()
+            bulk['y6', 0].wait_recv()
+            bulk['y6', 1].wait_recv()
             bulk['d7'] = c_partner(7)
             scores_rows(2 * pp[7] + half)
             bulk['d7'].wait_recv()
@@ -413,8 +425,8 @@
                 p2 = ET[1, 2 * k + j // 2, rows, lanes]
                 a1 = (p1 * p1) * rv[j:j + 1] * v1
                 a2 = (p2 * p2) * rv[4 + j:5 + j] * v2
-                Hs[0, rows, j * L:(j + 1) * L] = (p1 - a2).astype(BF16)
-                Hs[1, rows, j * L:(j + 1) * L] = (p2 - a1).astype(BF16)
+                Hs[0, j, rows] = (p1 - a2).astype(BF16)
+                Hs[1, j, rows] = (p2 - a1).astype(BF16)
 
     form_cols(H.at[0], 0)
     gsum[...] = jnp.zeros_like(gsum)
@@ -422,7 +434,7 @@
     def two(i, carry):
         for s in range(2):
             k = 2 * i + s
-            t = [jnp.dot(H[s, v], zall[v, pl.ds(2 * k, 2)].reshape(B, -1), preferred_element_type=F32) for v in range(2)]
+            t = [jnp.dot(slabs(H.at[s], v), zall[v, pl.ds(2 * k, 2)].reshape(B, -1), preferred_element_type=F32) for v in range(2)]
             gsum[...] += t[0] + t[1]
             form_cols(H.at[1 - s], lax.rem(k + 1, nd))
         return carry
@@ -453,13 +465,13 @@
                        sds((2, B, L), F32), sds((4, B, L), F32), sds((2, B, dim), F32)),
             in_specs=[HBM] * 3, out_specs=(VM,) * 9,
             scratch_shapes=[
-                pltpu.VMEM((2, B, B), F32), pltpu.VMEM((2, B, B), F32), pltpu.VMEM((2, 2, B, B), BF16),
+                pltpu.VMEM((2, B, B), F32), pltpu.VMEM((2, B, B), F32), pltpu.VMEM((2, 2, 4, B, L), BF16),
                 pltpu.VMEM((nd, 8, L), F32),
                 pltpu.VMEM((ITERS, 16, L), F32), pltpu.VMEM((ITERS, nd, 16, L), F32),
                 pltpu.VMEM((ITERS, 16, L), F32), pltpu.VMEM((ITERS, np_, 16, L), F32),
                 DMA((6,)), DMA((ITERS, nd)), DMA((ITERS, nd)), DMA((ITERS, np_)), DMA((ITERS, np_)),
                 DMA((np_,)), DMA((np_,)), DMA((nd,)), DMA((nd,)),
-                DMA((12,)), DMA((12,)), DMA((7,)), DMA((7,)), DMA((np_,)), DMA((np_,))],
+                DMA((12,)), DMA((12,)), DMA((10,)), DMA((10,)), DMA((np_,)), DMA((np_,))],
             compiler_params=pltpu.CompilerParams(collective_id=0, has_side_effects=True, vmem_limit_bytes=10 << 20),
             name='sinkhorn',
         )(*[pltpu.with_memory_space_constraint(a, pltpu.HBM) for a in (emb_one, emb_two, protos)])
@@ -468,7 +480,7 @@
             out_shape=(sds((B, B), F32), sds((B, B), F32), sds((1, 1), F32),
                        sds((B, dim), F32), sds((B, dim), F32), sds((B, dim), F32)),
             in_specs=[VM] * 9, out_specs=(ANY, ANY, VM, ANY, ANY, ANY),
-            scratch_shapes=[pltpu.VMEM((2, 2, B, B), BF16), pltpu.VMEM((2, B, B), F32),
+            scratch_shapes=[pltpu.VMEM((2, 2, 4, B, L), BF16), pltpu.VMEM((2, B, B), F32),
                             pltpu.VMEM((2, B, dim), F32), pltpu.VMEM((B, dim), F32), DMA((5,))],
             compiler_params=pltpu.CompilerParams(vmem_limit_bytes=17 << 20),
             name='grads',

time: 45.5 us -> 43.5 us (0.956)
  Pallas kernels: 44.5 us -> 42.8 us
    pallas_call x1, Pallas kernels: 37.5 us -> 36.4 us  [local_step(): pl.pallas_call(functools.partial(sinkhorn_kernel, np_, nd), out_shape=(sd...]
    pallas_call x1, Pallas kernels: 6.99 us -> 6.37 us  [local_step(): pl.pallas_call(functools.partial(grads_kernel, np_, nd), out_shape=(sds((...]
where the time goes in v4:
time: 43.5 us; the launch traced here: 43.4 us
  Pallas kernels  42.8 us (98%)
  between operations  0.64 us (1%)
    pallas_call x1, Pallas kernels, local_step(): pl.pallas_call(functools.partial(sinkhorn_kernel, np_, nd), out_shape=(sd...  36.4 us
    pallas_call x1, Pallas kernels, local_step(): pl.pallas_call(functools.partial(grads_kernel, np_, nd), out_shape=(sds((...  6.37 us

profile of v4, /device:TPU:1, one launch (start us, length us, event | category | flops | bytes accessed | tf_op | source)
XLA Modules:
  0.0 43.4 jit_solution(13252074504045556677)
XLA Ops:
  0.6 36.4 %sinkhorn.1 = (bf16[2,8,256,256]{3,2,1,0:T(8,128)(2,1)S(1)}, bf16[16,256,256]{2,1,0:T(8,128)(2,1)S(1)}, f32[2,16,512,256]{3,2,1,0:T(8,128)S(1)}, f32[2,8,512,256...) custom-call(bf16[512,256]{1,0:T(8,128)(2,1)} %z1.1, ...), custom_call_target="tpu_custom_call" | custom-call | tf_op jit(solution)/shard_map/sinkhorn/pallas_call | solution.py:460
  37.0 6.4 %grads.1 = (f32[512,512]{1,0:T(8,128)}, f32[512,512]{1,0:T(8,128)}, f32[1,1]{1,0:T(1,128)}, f32[512,256]{1,0:T(8,128)}, f32[512,256]{1,0:T(8,128)}, /*index=5*/f32[512,256]{1,0:T(8,128)}) custom-call(bf16[2,8,256,256]{3,2,1,0:T(8,128)(2,1)S(1)} %get-tuple-element.21.zall, bf16[16,256,256]{2,1,0:T(8,128)(2,1)S(1)} %get-tuple-element.22.call, ...), custom_call_target="tpu_custom_call" | custom-call | tf_op jit(solution)/shard_map/grads/pallas_call | solution.py:478

commit v5 on v4

--- a/solution.py
+++ b/solution.py
@@ -17,7 +17,7 @@
 HB = 256
 L = 128
 CH = 64
-EARLY = 4
+EARLY = 6
 RC = 16
 NT = (((1,), (1,)), ((), ()))
 
@@ -90,8 +90,8 @@
 
 
 def sinkhorn_kernel(np_, nd, z1, z2, c, zall, call, E, ET, rowv, vvec, vrep, ucol, G,
-                    T, A, H, dall, ctx, crx, rtx, rrx,
-                    lsem, cs, cr, rs, rr, vs, vr, us, ur, zs, zr, gs, gr, ds_, dr_):
+                    T, A, H, dall, ctx, crx, rtx, rrx, dtx, drx, ttx, trx,
+                    lsem, cs, cr, rs, rr, vs, vr, us, ur, ts, tr, zs, zr, gs, gr, ds_, dr_):
     p = lax.axis_index('proto')
     d = lax.axis_index('data')
     total_rows = nd * B
@@ -134,11 +134,11 @@
         ref = zall.at[v, nb]
         return send(ref, ref, zs.at[slot], zr.at[slot], 0, 1)
 
-    def c_send(slot, q, pj, part=None):
-        ref = call.at[2 * q + half]
-        if part is not None:
-            ref = ref.at[part * L:(part + 1) * L]
-        return send(ref, ref, gs.at[slot], gr.at[slot], pj, 0)
+    quarter = pl.ds(pl.multiple_of(d // 2 * L, L), L)
+
+    def c_send(slot, q, pj, dj=0, whole=False):
+        ref = call.at[2 * q + half] if whole else call.at[2 * q + half, quarter]
+        return send(ref, ref, gs.at[slot], gr.at[slot], pj, dj)
 
     def c_partner(j):
         ref = call.at[2 * pp[j] + half]
@@ -194,15 +194,24 @@
 
     bulk = {}
 
+    def c_x(j):
+        bulk['x', j] = c_send(7 + j, pp[j], 0, 2)
+
+    def have(*keys):
+        for key in keys:
+            bulk[key].wait_recv()
+
+    def hand_on(j):
+        bulk['d', j] = c_partner(j)
+
     def background(it, along_data):
         if it == 0 and along_data:
-            bulk['y0'] = c_send(0, p, 1)
-            bulk['z4', 0] = c_send(2, p, 4, 0)
-            bulk['z2'] = c_send(1, p, 2)
+            bulk['y', 0] = c_send(0, p, 1, whole=True)
+            bulk['z', 2] = c_send(1, p, 2)
+            bulk['z', 4] = c_send(2, p, 4)
             bulk['zx', 0] = z_x(0)
-            for v in range(2):
-                for h in range(2):
-                    bulk['zp', v, h] = z_partner(4 + 2 * v + h, v, 2 * d + h)
+            for i in range(4):
+                bulk['zp', i] = z_partner(4 + i, i // 2, 2 * d + i % 2)
             for v in range(2):
                 for ck in range(B // CH):
                     rows = pl.ds(ck * CH, CH)
@@ -214,85 +223,96 @@
                 T[v] = lax.dot_general(own_protos(), own_images(v), NT, preferred_element_type=F32) * LOG2E_TAU
         elif it == 0:
             bulk['zx', 1] = z_x(1)
-            bulk['y0'].wait_recv()
-            bulk['d1'] = c_partner(1)
-            bulk['z2'].wait_recv()
-            bulk['y2'] = c_send(4, pp[2], 1)
-            bulk['d2'] = c_partner(2)
+            have(('z', 2))
+            c_x(2)
+            bulk['y', 2] = c_send(4, pp[2], 1)
+            have(('y', 0))
+            hand_on(1)
+            have(('z', 4))
+            bulk['y', 4] = c_send(5, pp[4], 1)
         elif it == 1 and along_data:
-            bulk['z4', 1] = c_send(3, p, 4, 1)
-            bulk['z6', 0] = c_send(7, p, 6, 0)
+            bulk['z', 6] = c_send(3, p, 6)
+            c_x(4)
+            have(('y', 2))
+            c_x(3)
             bulk['zx', 2] = z_x(2)
+            have(('y', 4))
+            c_x(5)
             for i in range(8):
                 ucol[2 + i // 4, (i % 4) * L:(i % 4 + 1) * L] = jnp.broadcast_to(
                     row_to_col(eye, dscale[i:i + 1]), (L, L))
             scores_rows(2 * p)
             scores_rows(2 * p + 1)
+            have(('x', 2))
+            hand_on(2)
             scores_rows(2 * pp[1] + half)
         elif it == 1:
-            bulk['zx', 3] = z_x(3)
-            bulk['z4', 0].wait_recv()
-            bulk['z4', 1].wait_recv()
-            bulk['y4'] = c_send(5, pp[4], 1)
-            bulk['d4'] = c_partner(4)
-            bulk['y2'].wait_recv()
-            bulk['d3'] = c_partner(3)
+            have(('x', 4))
+            hand_on(4)
+            have(('d', 1))
+            scores_rows(2 * pp[1] + other)
             scores_rows(2 * pp[2] + half)
-            for j in (1, 2):
-                bulk['d%d' % j].wait_recv()
-                scores_rows(2 * pp[j] + other)
-            for v in range(2):
-                for h in range(2):
-                    bulk['zp', v, h].wait_recv()
+            have(('d', 2))
+            scores_rows(2 * pp[2] + other)
+            have(('z', 6))
+            c_x(6)
+            bulk['y', 6] = c_send(6, pp[6], 1)
+            have(('zp', 0), ('zp', 1), ('zp', 2), ('zp', 3))
             scores_cols(2 * dp[1])
             scores_cols(2 * dp[1] + 1)
-            scores_rows(2 * pp[4] + half)
-            scores_rows(2 * pp[3] + half)
-            bulk['z6', 0].wait_recv()
-            bulk['y6', 0] = c_send(6, pp[6], 1, 0)
             for v in range(2):
                 for h in range(2):
                     for j in range(2):
                         lanes = slice(j * L, (j + 1) * L)
                         k = 4 * v + 2 * h + j
                         ET[v, 2 * d + h, :, lanes] = ET[v, 2 * d + h, :, lanes] * dscale[k:k + 1]
+            scores_rows(2 * pp[4] + half)
         elif it == 2 and along_data:
-            bulk['z6', 1] = c_send(8, p, 6, 1)
-            for j in (4, 3):
-                bulk['d%d' % j].wait_recv()
+            bulk['zx', 3] = z_x(3)
+            have(('x', 3))
+            hand_on(3)
+            have(('x', 5))
+            hand_on(5)
+            have(('d', 4))
+            scores_rows(2 * pp[4] + other)
+            for i in range(3):
+                have(('zx', i))
+                bulk['zf', i] = z_partner(8 + i, i // 2, 2 * dp[2] + i % 2)
+            scores_rows(2 * pp[3] + half)
+            scores_rows(2 * pp[5] + half)
+        elif it == 2:
+            have(('y', 6))
+            c_x(7)
+            have(('x', 6))
+            hand_on(6)
+            have(('zx', 3))
+            bulk['zf', 3] = z_partner(11, 1, 2 * dp[2] + 1)
+            for j in (3, 5):
+                have(('d', j))
                 scores_rows(2 * pp[j] + other)
-            for i in range(4):
-                bulk['zx', i].wait_recv()
-                bulk['zf', i] = z_partner(8 + i, i // 2, 2 * dp[2] + i % 2)
             scores_cols(2 * dp[2])
             scores_cols(2 * dp[2] + 1)
-        elif it == 2:
-            bulk['z6', 1].wait_recv()
-            bulk['y6', 1] = c_send(9, pp[6], 1, 1)
-            bulk['d6'] = c_partner(6)
-            bulk['y4'].wait_recv()
-            bulk['d5'] = c_partner(5)
-            for i in range(4):
-                bulk['zf', i].wait_recv()
+            have(('zf', 0), ('zf', 1), ('zf', 2), ('zf', 3))
             scores_cols(2 * dp[3])
             scores_cols(2 * dp[3] + 1)
-            for j in (6, 5):
-                scores_rows(2 * pp[j] + half)
-                bulk['d%d' % j].wait_recv()
-                scores_rows(2 * pp[j] + other)
-        else:
-            for i in range(8):
-                ucol[i // 4, (i % 4) * L:(i % 4 + 1) * L] = jnp.broadcast_to(
-                    row_to_col(eye, useg[i:i + 1]), (L, L))
-            for cp in vcps:
-                cp.wait_recv()
-            dz_blocks(E, vvec, ucol, H, call, G, p, 0, EARLY, True)
-            bulk['y6', 0].wait_recv()
-            bulk['y6', 1].wait_recv()
-            bulk['d7'] = c_partner(7)
+            have(('x', 7))
+            hand_on(7)
+            scores_rows(2 * pp[6] + half)
+            have(('d', 6))
+            scores_rows(2 * pp[6] + other)
             scores_rows(2 * pp[7] + half)
-            bulk['d7'].wait_recv()
+            have(('d', 7))
             scores_rows(2 * pp[7] + other)
+
+    def sum_tiles(own, parts, cps):
+        tot = own[...]
+        for j, cp in zip(range(1, np_), cps):
+            cp.wait_recv()
+            tot = tot + parts[j]
+        return tot
+
+    def row_tile(own, parts, ss, rs_):
+        return [send(own, parts.at[j], ss.at[j], rs_.at[j], j, 0) for j in range(1, np_)]
 
     for it in range(ITERS):
         last = it == ITERS - 1
@@ -301,6 +321,8 @@
         nc = 8
         if it == 1:
             nc = 16
+            dfull = sum_tiles(dtx, drx, dcps)
+            dscale = inv_scale / dfull
             ctx[it, 8:16] = dscale
         cps = [send(ctx.at[it, 0:nc], crx.at[it, j, 0:nc], cs.at[it, j], cr.at[it, j], 0, j) for j in range(1, nd)]
         background(it, True)
@@ -313,43 +335,42 @@
             for j in range(1, nd):
                 dall[dp[j]] = crx[it, j, 8:16]
         vt = 1.0 / (total_protos * ctot)
-        if last:
-            vvec[p] = vt
-            vcps = [send(vvec.at[p], vvec.at[p], vs.at[j], vr.at[j], j, 0) for j in range(1, np_)]
         for v in range(2):
             for i in range(4):
                 vrep[v, i * L:(i + 1) * L] = jnp.broadcast_to(row_to_col(eye, vt[4 * v + i:4 * v + i + 1]), (L, L))
         for v in range(2):
             racc = [jnp.zeros((8, L), F32) for _ in range(4)]
-            tacc = [jnp.zeros((8, L), F32) for _ in range(4)]
             for ck in range(B // CH):
                 rows = pl.ds(ck * CH, CH)
                 wv = vrep[v, rows]
                 for j in range(4):
-                    lanes = slice(j * L, (j + 1) * L)
-                    m = A[v, rows, lanes] * wv
+                    m = A[v, rows, j * L:(j + 1) * L] * wv
                     racc[j] = racc[j] + jnp.sum(m.reshape(CH // 8, 8, L), axis=0)
-                    if last:
-                        mt = m * T[1 - v, rows, lanes]
-                        tacc[j] = tacc[j] + jnp.sum(mt.reshape(CH // 8, 8, L), axis=0)
             for j in range(4):
                 rtx[it, 4 * v + j:4 * v + j + 1] = jnp.sum(racc[j], axis=0, keepdims=True)
-                if last:
-                    rtx[it, 8 + 4 * v + j:8 + 4 * v + j + 1] = jnp.sum(tacc[j], axis=0, keepdims=True)
+        cps = row_tile(rtx.at[it], rrx.at[it], rs.at[it], rr.at[it])
         if it == 0:
             for i in range(8):
-                rtx[it, 8 + i:9 + i] = dsum[i]
-        nrow = 8 if it == 1 else 16
-        cps = [send(rtx.at[it, 0:nrow], rrx.at[it, j, 0:nrow], rs.at[it, j], rr.at[it, j], j, 0) for j in range(1, np_)]
+                dtx[i:i + 1] = dsum[i]
+            dcps = row_tile(dtx, drx, ts.at[0], tr.at[0])
+        if last:
+            vvec[p] = vt
+            vcps = [send(vvec.at[p], vvec.at[p], vs.at[j], vr.at[j], j, 0) for j in range(1, np_)]
+            for v in range(2):
+                tacc = [jnp.zeros((8, L), F32) for _ in range(4)]
+                for ck in range(B // CH):
+                    rows = pl.ds(ck * CH, CH)
+                    wv = vrep[v, rows]
+                    for j in range(4):
+                        lanes = slice(j * L, (j + 1) * L)
+                        mt = A[v, rows, lanes] * wv * T[1 - v, rows, lanes]
+                        tacc[j] = tacc[j] + jnp.sum(mt.reshape(CH // 8, 8, L), axis=0)
+                for j in range(4):
+                    ttx[4 * v + j:4 * v + j + 1] = jnp.sum(tacc[j], axis=0, keepdims=True)
+            tcps = row_tile(ttx, trx, ts.at[1], tr.at[1])
         background(it, False)
-        rtot = rtx[it, 0:nrow]
-        for j, cp in zip(range(1, np_), cps):
-            cp.wait_recv()
-            rtot = rtot + rrx[it, j, 0:nrow]
-        if it == 0:
-            dfull = rtot[8:16]
-            dscale = inv_scale / dfull
-        u_tile = 1.0 / (total_rows * rtot[0:8])
+        rtot = sum_tiles(rtx.at[it], rrx.at[it], cps)
+        u_tile = 1.0 / (total_rows * rtot)
         if not last:
             for v in range(2):
                 cols = []
@@ -365,15 +386,21 @@
                     crow[4 * v + i] = col_to_row(eye, jnp.concatenate(cols[per * i:per * (i + 1)], axis=0))
 
     w = total_rows * u_tile
+    useg = w * inv_scale / (dscale * dscale)
+    rowv[d, 0:8] = useg
+    ucps = [send(rowv.at[d, 0:8], rowv.at[d, 0:8], us.at[0, j], ur.at[0, j], 0, j) for j in range(1, nd)]
+    for i in range(8):
+        ucol[i // 4, (i % 4) * L:(i % 4 + 1) * L] = jnp.broadcast_to(row_to_col(eye, useg[i:i + 1]), (L, L))
+    ttot = sum_tiles(ttx, trx, tcps)
     logd = jnp.log(dfull)
     swapped = jnp.concatenate([logd[4:8], logd[0:4]], axis=0)
-    terms = w * rtot[8:16] * LN2 - (w * rtot[0:8]) * swapped
+    terms = w * ttot * LN2 - (w * rtot) * swapped
     tot = jnp.sum(jnp.sum(terms, axis=1, keepdims=True), axis=0, keepdims=True)
-    useg = w * inv_scale / (dscale * dscale)
-    rowv[d, 0:8] = useg
     rowv[d, 8:16] = jnp.broadcast_to(tot, (8, L))
-    ucps = [send(rowv.at[d], rowv.at[d], us.at[j], ur.at[j], 0, j) for j in range(1, nd)]
-    background(ITERS, True)
+    ucps += [send(rowv.at[d, 8:16], rowv.at[d, 8:16], us.at[1, j], ur.at[1, j], 0, j) for j in range(1, nd)]
+    for cp in vcps:
+        cp.wait_recv()
+    dz_blocks(E, vvec, ucol, H, call, G, p, 0, EARLY, True)
     for cp in ucps:
         cp.wait_recv()
     for cp in pend:
@@ -468,10 +495,11 @@
                 pltpu.VMEM((2, B, B), F32), pltpu.VMEM((2, B, B), F32), pltpu.VMEM((2, 2, 4, B, L), BF16),
                 pltpu.VMEM((nd, 8, L), F32),
                 pltpu.VMEM((ITERS, 16, L), F32), pltpu.VMEM((ITERS, nd, 16, L), F32),
-                pltpu.VMEM((ITERS, 16, L), F32), pltpu.VMEM((ITERS, np_, 16, L), F32),
+                pltpu.VMEM((ITERS, 8, L), F32), pltpu.VMEM((ITERS, np_, 8, L), F32),
+                pltpu.VMEM((8, L), F32), pltpu.VMEM((np_, 8, L), F32), pltpu.VMEM((8, L), F32), pltpu.VMEM((np_, 8, L), F32),
                 DMA((6,)), DMA((ITERS, nd)), DMA((ITERS, nd)), DMA((ITERS, np_)), DMA((ITERS, np_)),
-                DMA((np_,)), DMA((np_,)), DMA((nd,)), DMA((nd,)),
-                DMA((12,)), DMA((12,)), DMA((10,)), DMA((10,)), DMA((np_,)), DMA((np_,))],
+                DMA((np_,)), DMA((np_,)), DMA((2, nd)), DMA((2, nd)), DMA((2, np_)), DMA((2, np_)),
+                DMA((12,)), DMA((12,)), DMA((15,)), DMA((15,)), DMA((np_,)), DMA((np_,))],
             compiler_params=pltpu.CompilerParams(collective_id=0, has_side_effects=True, vmem_limit_bytes=10 << 20),
             name='sinkhorn',
         )(*[pltpu.with_memory_space_constraint(a, pltpu.HBM) for a in (emb_one, emb_two, protos)])

time: 43.5 us -> 42 us (0.966)
  Pallas kernels: 42.8 us -> 41.2 us
    pallas_call x1, Pallas kernels: 6.37 us -> 5.12 us  [local_step(): pl.pallas_call(functools.partial(grads_kernel, np_, nd), out_shape=(sds((...]
where the time goes in v5:
time: 42 us; the launch traced here: 41.8 us
  Pallas kernels  41.2 us (98%)
  between operations  0.64 us (2%)
    pallas_call x1, Pallas kernels, local_step(): pl.pallas_call(functools.partial(sinkhorn_kernel, np_, nd), out_shape=(sd...  36.1 us
    pallas_call x1, Pallas kernels, local_step(): pl.pallas_call(functools.partial(grads_kernel, np_, nd), out_shape=(sds((...  5.12 us

profile of v5, /device:TPU:1, one launch (start us, length us, event | category | flops | bytes accessed | tf_op | source)
XLA Modules:
  0.0 41.8 jit_solution(12069797912672028382)
XLA Ops:
  0.6 36.1 %sinkhorn.1 = (bf16[2,8,256,256]{3,2,1,0:T(8,128)(2,1)S(1)}, bf16[16,256,256]{2,1,0:T(8,128)(2,1)S(1)}, f32[2,16,512,256]{3,2,1,0:T(8,128)S(1)}, f32[2,8,512,256...) custom-call(bf16[512,256]{1,0:T(8,128)(2,1)} %z1.1, ...), custom_call_target="tpu_custom_call" | custom-call | tf_op jit(solution)/shard_map/sinkhorn/pallas_call | solution.py:487
  36.7 5.1 %grads.1 = (f32[512,512]{1,0:T(8,128)}, f32[512,512]{1,0:T(8,128)}, f32[1,1]{1,0:T(1,128)}, f32[512,256]{1,0:T(8,128)}, f32[512,256]{1,0:T(8,128)}, /*index=5*/f32[512,256]{1,0:T(8,128)}) custom-call(bf16[2,8,256,256]{3,2,1,0:T(8,128)(2,1)S(1)} %get-tuple-element.21.zall, bf16[16,256,256]{2,1,0:T(8,128)(2,1)S(1)} %get-tuple-element.22.call, ...), custom_call_target="tpu_custom_call" | custom-call | tf_op jit(solution)/shard_map/grads/pallas_call | solution.py:506

commit v6 on v5

--- a/solution.py
+++ b/solution.py
@@ -17,7 +17,6 @@
 HB = 256
 L = 128
 CH = 64
-EARLY = 6
 RC = 16
 NT = (((1,), (1,)), ((), ()))
 
@@ -64,21 +63,20 @@
             H[1, j, rows] = (p2 - a1).astype(BF16)
 
 
-def dz_blocks(E, vvec, ucol, H, call, G, p, lo, hi, first):
-    form_rows(E, vvec, ucol, H.at[0], xor2(p, lo))
-    if first:
-        G[...] = jnp.zeros_like(G)
+def dz_blocks(E, vvec, ucol, H, call, G, p, n):
+    form_rows(E, vvec, ucol, H.at[0], p)
+    G[...] = jnp.zeros_like(G)
 
     def two(i, carry):
         for s in range(2):
-            j = lo + 2 * i + s
+            j = 2 * i + s
             q = xor2(p, j)
             for v in range(2):
                 G[v] += times_block(H.at[s], v, call, q)
             form_rows(E, vvec, ucol, H.at[1 - s], xor2(p, lax.rem(j + 1, 8)))
         return carry
 
-    lax.fori_loop(0, (hi - lo) // 2, two, 0)
+    lax.fori_loop(0, n // 2, two, 0)
 
 
 def slabs(H, v):
@@ -400,7 +398,7 @@
     ucps += [send(rowv.at[d, 8:16], rowv.at[d, 8:16], us.at[1, j], ur.at[1, j], 0, j) for j in range(1, nd)]
     for cp in vcps:
         cp.wait_recv()
-    dz_blocks(E, vvec, ucol, H, call, G, p, 0, EARLY, True)
+    dz_blocks(E, vvec, ucol, H, call, G, p, np_)
     for cp in ucps:
         cp.wait_recv()
     for cp in pend:
@@ -408,7 +406,7 @@
 
 
 def grads_kernel(np_, nd, zall, call, E, ET, rowv, vvec, vrep, ucol, G, q1, q2, loss, g1, g2, gp,
-                 H, qbuf, gbuf, gsum, sem):
+                 H, qbuf, gsum, sem):
     p = lax.axis_index('proto')
     d = lax.axis_index('data')
     total_rows = nd * B
@@ -435,9 +433,7 @@
     for cp in out:
         cp.start()
 
-    gbuf[0:2] = G[...]
-    dz_blocks(E, vvec, ucol, H, call, gbuf, p, EARLY, np_, False)
-    gout = [pltpu.make_async_copy(gbuf.at[0], g1, sem.at[2]), pltpu.make_async_copy(gbuf.at[1], g2, sem.at[3])]
+    gout = [pltpu.make_async_copy(G.at[0], g1, sem.at[2]), pltpu.make_async_copy(G.at[1], g2, sem.at[3])]
     for cp in gout:
         cp.start()
 
@@ -509,7 +505,7 @@
                        sds((B, dim), F32), sds((B, dim), F32), sds((B, dim), F32)),
             in_specs=[VM] * 9, out_specs=(ANY, ANY, VM, ANY, ANY, ANY),
             scratch_shapes=[pltpu.VMEM((2, 2, 4, B, L), BF16), pltpu.VMEM((2, B, B), F32),
-                            pltpu.VMEM((2, B, dim), F32), pltpu.VMEM((B, dim), F32), DMA((5,))],
+                            pltpu.VMEM((B, dim), F32), DMA((5,))],
             compiler_params=pltpu.CompilerParams(vmem_limit_bytes=17 << 20),
             name='grads',
         )(*mid)

time: 42 us -> 41.9 us (level)
    pallas_call x1, Pallas kernels: 5.12 us -> 3.98 us  [local_step(): pl.pallas_call(functools.partial(grads_kernel, np_, nd), out_shape=(sds((...]
    pallas_call x1, Pallas kernels: 36.1 us -> 37.1 us  [local_step(): pl.pallas_call(functools.partial(sinkhorn_kernel, np_, nd), out_shape=(sd...]
where the time goes in v6:
time: 41.9 us; the launch traced here: 41.7 us
  Pallas kernels  41.1 us (98%)
  between operations  0.64 us (2%)
    pallas_call x1, Pallas kernels, local_step(): pl.pallas_call(functools.partial(sinkhorn_kernel, np_, nd), out_shape=(sd...  37.1 us
    pallas_call x1, Pallas kernels, local_step(): pl.pallas_call(functools.partial(grads_kernel, np_, nd), out_shape=(sds((...  3.98 us

profile of v6, /device:TPU:1, one launch (start us, length us, event | category | flops | bytes accessed | tf_op | source)
XLA Modules:
  0.0 41.7 jit_solution(7894109118796533551)
XLA Ops:
  0.6 37.1 %sinkhorn.1 = (bf16[2,8,256,256]{3,2,1,0:T(8,128)(2,1)S(1)}, bf16[16,256,256]{2,1,0:T(8,128)(2,1)S(1)}, f32[2,16,512,256]{3,2,1,0:T(8,128)S(1)}, f32[2,8,512,256...) custom-call(bf16[512,256]{1,0:T(8,128)(2,1)} %z1.1, ...), custom_call_target="tpu_custom_call" | custom-call | tf_op jit(solution)/shard_map/sinkhorn/pallas_call | solution.py:483
  37.7 4.0 %grads.1 = (f32[512,512]{1,0:T(8,128)}, f32[512,512]{1,0:T(8,128)}, f32[1,1]{1,0:T(1,128)}, f32[512,256]{1,0:T(8,128)}, f32[512,256]{1,0:T(8,128)}, /*index=5*/f32[512,256]{1,0:T(8,128)}) custom-call(bf16[2,8,256,256]{3,2,1,0:T(8,128)(2,1)S(1)} %get-tuple-element.21.zall, bf16[16,256,256]{2,1,0:T(8,128)(2,1)S(1)} %get-tuple-element.22.call, ...), custom_call_target="tpu_custom_call" | custom-call | tf_op jit(solution)/shard_map/grads/pallas_call | solution.py:502

commit v7 on v6

--- a/solution.py
+++ b/solution.py
@@ -76,7 +76,13 @@
             form_rows(E, vvec, ucol, H.at[1 - s], xor2(p, lax.rem(j + 1, 8)))
         return carry
 
-    lax.fori_loop(0, n // 2, two, 0)
+    lax.fori_loop(0, n // 2 - 1, two, 0)
+    qa, qb = xor2(p, n - 2), xor2(p, n - 1)
+    for v in range(2):
+        G[v] += times_block(H.at[0], v, call, qa)
+    form_rows(E, vvec, ucol, H.at[1], qb)
+    for v in range(2):
+        G[v] += times_block(H.at[1], v, call, qb)
 
 
 def slabs(H, v):
@@ -462,7 +468,12 @@
             form_cols(H.at[1 - s], lax.rem(k + 1, nd))
         return carry
 
-    lax.fori_loop(0, nd // 2, two, 0)
+    lax.fori_loop(0, nd // 2 - 1, two, 0)
+    for s, k in ((0, nd - 2), (1, nd - 1)):
+        t = [jnp.dot(slabs(H.at[s], v), zall[v, 2 * k:2 * k + 2].reshape(B, -1), preferred_element_type=F32) for v in range(2)]
+        gsum[...] += t[0] + t[1]
+        if s == 0:
+            form_cols(H.at[1], nd - 1)
     gout.append(pltpu.make_async_copy(gsum, gp, sem.at[4]))
     gout[-1].start()
     for cp in out + gout:

time: 41.9 us -> 42.2 us (level)
    pallas_call x1, Pallas kernels: 3.98 us -> 4.61 us  [local_step(): pl.pallas_call(functools.partial(grads_kernel, np_, nd), out_shape=(sds((...]
where the time goes in v7:
time: 42.2 us; the launch traced here: 42 us
  Pallas kernels  41.4 us (98%)
  between operations  0.64 us (2%)
    pallas_call x1, Pallas kernels, local_step(): pl.pallas_call(functools.partial(sinkhorn_kernel, np_, nd), out_shape=(sd...  36.8 us
    pallas_call x1, Pallas kernels, local_step(): pl.pallas_call(functools.partial(grads_kernel, np_, nd), out_shape=(sds((...  4.61 us

profile of v7, /device:TPU:1, one launch (start us, length us, event | category | flops | bytes accessed | tf_op | source)
XLA Modules:
  0.0 42.0 jit_solution(17687557415191179134)
XLA Ops:
  0.6 36.8 %sinkhorn.1 = (bf16[2,8,256,256]{3,2,1,0:T(8,128)(2,1)S(1)}, bf16[16,256,256]{2,1,0:T(8,128)(2,1)S(1)}, f32[2,16,512,256]{3,2,1,0:T(8,128)S(1)}, f32[2,8,512,256...) custom-call(bf16[512,256]{1,0:T(8,128)(2,1)} %z1.1, ...), custom_call_target="tpu_custom_call" | custom-call | tf_op jit(solution)/shard_map/sinkhorn/pallas_call | solution.py:494
  37.4 4.6 %grads.1 = (f32[512,512]{1,0:T(8,128)}, f32[512,512]{1,0:T(8,128)}, f32[1,1]{1,0:T(1,128)}, f32[512,256]{1,0:T(8,128)}, f32[512,256]{1,0:T(8,128)}, /*index=5*/f32[512,256]{1,0:T(8,128)}) custom-call(bf16[2,8,256,256]{3,2,1,0:T(8,128)(2,1)S(1)} %get-tuple-element.21.zall, bf16[16,256,256]{2,1,0:T(8,128)(2,1)S(1)} %get-tuple-element.22.call, ...), custom_call_target="tpu_custom_call" | custom-call | tf_op jit(solution)/shard_map/grads/pallas_call | solution.py:513
